TPU v7x, 256 devices: a whole 4x4x8 slice. The times are simulated.
256 devices in a mesh: depth: 8 (over y, core), lat: 32 (over z, x).
Axes of the slice: x: 4, y: 4, z: 8, core: 2. Of those that a mesh axis runs over, the one named last changes fastest.
Arguments:
- fields: float32 [8, 2, 2, 2, 512, 512], P('depth', None, None, None, 'lat'), may hold values from -6 to 6
- surface: float32 [2, 2, 2, 512, 512], P(None, None, None, 'lat'), may hold values from -6 to 6
- held_freqs: int32 [8, 2], P('depth'), may hold values from 8 to 63
- surface_freqs: int32 [2], replicated, may hold values from 8 to 63
- ref_slowness: float32 [8, 1, 2], P('depth'), may hold values from 0.6 to 1.2
- weights: float32 [8, 1, 512, 512], P('depth', None, 'lat'), may hold values from 0 to 1
- regions: int32 [8, 1, 512, 512], P('depth', None, 'lat'), may hold values from 0 to 7
- region_slowness: float32 [8, 1, 8], P('depth'), may hold values from 0.6 to 1.2
Outputs:
- fields_out: float32 [8, 2, 2, 2, 512, 512], P('depth', None, None, None, 'lat')
- image_out: float32 [8, 1, 16, 512, 512], P('depth', None, None, 'lat')
All inputs are finite; a program needn't handle non-finite values.
Results may differ from a plain program's by a relative error of at most 0.0003.
Values sent between devices are 32-bit elements; how exact they have to be, the bound alone decides.
No kernel may reach another device: no remote copies, remote signals or barrier semaphores. Data moves between devices by JAX's collectives and lax.ppermute only.
A program may use at most 64 MiB of HBM per device.

v0:
```python
import functools
import math

import jax
import jax.numpy as jnp
import ml_dtypes
import numpy as np
from jax import lax
from jax.experimental import pallas as pl
from jax.experimental.pallas import tpu as pltpu
from jax.sharding import PartitionSpec as P

LAGS = 16
HALF = LAGS // 2
REGIONS = 8
CHUNK = 16
LANES = 128
INTERPRET = False

omega_step = 0.04
depth_step = 1.0

COS_TERMS = [(-1.0) ** n / math.factorial(2 * n) for n in range(13)]
SIN_TERMS = [(-1.0) ** n / math.factorial(2 * n + 1) for n in range(13)]


def polynomial(value, terms):
    total = jnp.full_like(value, terms[-1])
    for term in terms[-2::-1]:
        total = total * value + term
    return total


def transform_table(length):
    index = np.arange(length)
    angle = 2.0 * np.pi * (index[:, None] * index[None, :] % length) / length
    table = np.concatenate([np.cos(angle), np.sin(angle)], axis=1)
    lead = table.astype(ml_dtypes.bfloat16)
    trail = (table - lead.astype(np.float64)).astype(ml_dtypes.bfloat16)
    return lead, trail


def two_parts(value):
    lead = value.astype(jnp.bfloat16)
    return lead, (value - lead.astype(jnp.float32)).astype(jnp.bfloat16)


def dot(left, right):
    return jnp.dot(left, right, preferred_element_type=jnp.float32)


def dot_rows(value, lead_ref, trail_ref):
    lead, trail = two_parts(value)
    return dot(lead, lead_ref[...]) + (dot(trail, lead_ref[...]) + dot(lead, trail_ref[...]))


def dot_columns(lead_ref, trail_ref, value, length):
    lead, trail = two_parts(value)
    results = []
    for part in range(2):
        at = pl.ds(part * length, length)
        results.append(
            dot(lead_ref[:, at], lead) + (dot(lead_ref[:, at], trail) + dot(trail_ref[:, at], lead))
        )
    return results


def swap_chunks(pieces):
    pieces = list(pieces)
    lane = lax.broadcasted_iota(jnp.int32, pieces[0].shape, 1)
    for bit in (1, 2, 4):
        upper = (lane // (CHUNK * bit)) % 2 == 1
        for low in range(8):
            if low & bit:
                continue
            first, second = pieces[low], pieces[low | bit]
            pieces[low] = jnp.where(upper, pltpu.roll(second, CHUNK * bit, 1), first)
            pieces[low | bit] = jnp.where(upper, second, pltpu.roll(first, LANES - CHUNK * bit, 1))
    return pieces


def rows_to_blocks(value, lead_ref, trail_ref, out_ref, rows):
    length = value.shape[1]
    half = value.shape[0] // 2
    both = dot_rows(value, lead_ref, trail_ref)
    cos_part, sin_part = both[:, :length], both[:, length:]
    spectrum = (cos_part[:half] + sin_part[half:], cos_part[half:] - sin_part[:half])
    for tile in range(length // LANES):
        lanes = slice(tile * LANES, (tile + 1) * LANES)
        pieces = [
            spectrum[part][group * rows : (group + 1) * rows, lanes]
            for part in range(2)
            for group in range(half // rows)
        ]
        for block, piece in enumerate(swap_chunks(pieces)):
            out_ref[pl.ds((tile * 8 + block) * rows, rows), :] = piece


def rows_kernel(field_ref, lead_ref, trail_ref, out_ref, *, rows):
    rows_to_blocks(field_ref[...], lead_ref, trail_ref, out_ref, rows)


def factor_kernel(freq_ref, slow_ref, block_ref, even_ref, odd_ref, *, length, col_length):
    shape = (length, LANES)
    row = lax.broadcasted_iota(jnp.int32, shape, 0)
    lane = lax.broadcasted_iota(jnp.int32, shape, 1)
    step_x, step_y = 2.0 * math.pi / length, 2.0 * math.pi / col_length
    wave_x = jnp.where(row < length // 2, row, row - length).astype(jnp.float32) * step_x
    col = block_ref[0] * CHUNK + lane % CHUNK
    wave_y = jnp.where(col < col_length // 2, col, col - col_length).astype(jnp.float32) * step_y
    squared = wave_x * wave_x + wave_y * wave_y
    omega = jnp.where((lane // CHUNK) % 2 == 0, freq_ref[0], freq_ref[1])
    is_source = (lane // (2 * CHUNK)) % 2 == 0
    is_real = lane < LANES // 2
    direction = jnp.where(is_source == is_real, 1.0, -1.0)
    for ref in range(2):
        base = omega * slow_ref[ref]
        gap = base * base - squared
        fade = jnp.exp(-jnp.sqrt(jnp.maximum(-gap, 0.0)) * depth_step)
        inside = jnp.maximum(gap, 0.0)
        even_ref[ref] = fade * polynomial(inside, COS_TERMS)
        odd_ref[ref] = direction * (fade * (jnp.sqrt(inside) * polynomial(inside, SIN_TERMS)))


def columns_kernel(in_ref, even_ref, odd_ref, lead_ref, trail_ref, out_ref):
    length = in_ref.shape[0]
    lane = lax.broadcasted_iota(jnp.int32, (length, LANES), 1)
    turn = jnp.where(lane < LANES // 2, 1.0, -1.0)
    cos_part, sin_part = dot_columns(lead_ref, trail_ref, in_ref[...], length)
    spectrum = cos_part + turn * pltpu.roll(sin_part, LANES // 2, 1)
    swapped = pltpu.roll(spectrum, LANES // 2, 1)
    shifted = [spectrum * even_ref[ref] + swapped * odd_ref[ref] for ref in range(2)]
    cos_part, sin_part = dot_columns(
        lead_ref, trail_ref, jnp.concatenate(shifted, axis=1), length
    )
    for ref in range(2):
        lanes = slice(ref * LANES, (ref + 1) * LANES)
        out_ref[:, lanes] = cos_part[:, lanes] - turn * pltpu.roll(
            sin_part[:, lanes], LANES // 2, 1
        )


def continued(in_ref, lens_ref, weight_ref, lead_ref, trail_ref, rows):
    length = lead_ref.shape[0]
    tiles = []
    for tile in range(length // LANES):
        column = []
        for ref in range(2):
            column += swap_chunks(
                [
                    in_ref[pl.ds((tile * 8 + block) * rows, rows), ref * LANES : (ref + 1) * LANES]
                    for block in range(8)
                ]
            )
        tiles.append(jnp.concatenate(column, axis=0))
    both = dot_rows(jnp.concatenate(tiles, axis=1), lead_ref, trail_ref)
    cos_part, sin_part = both[:, :length], both[:, length:]
    half = 4 * rows
    weight = weight_ref[...]
    real, imag = [], []
    for group in range(4):
        parts = []
        for ref in range(2):
            at_real = ref * 2 * half + group * rows
            at_imag = at_real + half
            parts.append(
                (
                    cos_part[at_real : at_real + rows] - sin_part[at_imag : at_imag + rows],
                    cos_part[at_imag : at_imag + rows] + sin_part[at_real : at_real + rows],
                )
            )
        mixed = [weight * parts[0][p] + (1.0 - weight) * parts[1][p] for p in range(2)]
        lens_cos = lens_ref[0, group % 2]
        lens_sin = lens_ref[1, group % 2] if group >= 2 else -lens_ref[1, group % 2]
        real.append(mixed[0] * lens_cos - mixed[1] * lens_sin)
        imag.append(mixed[0] * lens_sin + mixed[1] * lens_cos)
    return jnp.concatenate(real + imag, axis=0)


def turn_kernel(
    in_ref, lens_ref, weight_ref, surface_ref, last_ref, lead_ref, trail_ref, field_ref, out_ref, *, rows
):
    field = continued(in_ref, lens_ref, weight_ref, lead_ref, trail_ref, rows)
    field_ref[...] = field
    start = jnp.where(last_ref[0] == 1, surface_ref[...], field)
    rows_to_blocks(start, lead_ref, trail_ref, out_ref, rows)


def end_kernel(in_ref, lens_ref, weight_ref, lead_ref, trail_ref, field_ref, *, rows):
    field_ref[...] = continued(in_ref, lens_ref, weight_ref, lead_ref, trail_ref, rows)


def image_body(field_ref, above_ref, below_ref, base_ref, out_ref, padded_ref, rows):
    for index in range(8):
        padded_ref[index, pl.ds(0, HALF)] = above_ref[index]
        padded_ref[index, pl.ds(HALF, rows)] = field_ref[index]
        padded_ref[index, pl.ds(HALF + rows, HALF)] = below_ref[index]
    for lag in range(LAGS):
        offset = lag - HALF
        total = None if base_ref is None else base_ref[lag]
        for part in range(2):
            for freq in range(2):
                source = padded_ref[part * 4 + freq, pl.ds(HALF - offset, rows)]
                receiver = padded_ref[part * 4 + 2 + freq, pl.ds(HALF + offset, rows)]
                total = source * receiver if total is None else total + source * receiver
        out_ref[lag] = total


def image_first(field_ref, above_ref, below_ref, out_ref, padded_ref, *, rows):
    image_body(field_ref, above_ref, below_ref, None, out_ref, padded_ref, rows)


def image_second(field_ref, above_ref, below_ref, base_ref, out_ref, padded_ref, *, rows):
    image_body(field_ref, above_ref, below_ref, base_ref, out_ref, padded_ref, rows)


VMEM = pl.BlockSpec(memory_space=pltpu.VMEM)
SMEM = pl.BlockSpec(memory_space=pltpu.SMEM)


def call(kernel, name, in_specs, out_shapes, operands, flops, scratch=(), **params):
    many = len(out_shapes) > 1
    shapes = [jax.ShapeDtypeStruct(shape, jnp.float32) for shape in out_shapes]
    return pl.pallas_call(
        functools.partial(kernel, **params),
        name=name,
        in_specs=in_specs,
        out_specs=[VMEM] * len(shapes) if many else VMEM,
        out_shape=shapes if many else shapes[0],
        scratch_shapes=list(scratch),
        cost_estimate=pl.CostEstimate(flops=flops, bytes_accessed=1 << 20, transcendentals=0),
        compiler_params=pltpu.CompilerParams(vmem_limit_bytes=24 << 20),
        interpret=INTERPRET,
    )(*operands)


def exchanged(value):
    return lax.all_to_all(value, "lat", split_axis=0, concat_axis=0, tiled=True)


def shards(
    fields, surface, held_freqs, surface_freqs, ref_slowness, weights, regions, region_slowness
):
    lane_count = lax.axis_size("lat")
    sections = lax.axis_size("depth")
    rows, col_length = fields.shape[4], fields.shape[5]
    length = lane_count * rows
    table_y = [jnp.asarray(part) for part in transform_table(col_length)]
    table_x = table_y if length == col_length else [jnp.asarray(p) for p in transform_table(length)]
    flat = (8 * rows, col_length)
    block = lax.axis_index("lat").reshape(1)
    at_end = lax.axis_index("depth") == sections - 1

    region_ids = jnp.arange(REGIONS, dtype=jnp.int32)
    matches = (regions[0, 0][None] == region_ids[:, None, None]).astype(jnp.float32)
    cell_slowness = jnp.sum(matches * region_slowness[0, 0][:, None, None], axis=0)
    weight = weights[0, 0]
    slow = ref_slowness[0, 0]
    blend = weight * slow[0] + (1.0 - weight) * slow[1]
    lens_gap = cell_slowness - blend
    upward = [(s, (s - 1) % sections) for s in range(sections)]
    slow_rows = jnp.broadcast_to(slow[:, None, None], (2, 4, col_length)).reshape(8, col_length)
    passed = lax.ppermute(jnp.concatenate([lens_gap, weight, slow_rows], axis=0), "depth", upward)
    next_gap, next_weight = passed[:rows], passed[rows : 2 * rows]
    next_slow = passed[2 * rows :: 4, 0]

    omega = held_freqs[0].astype(jnp.float32) * omega_step
    next_omega = jnp.where(at_end, surface_freqs.astype(jnp.float32) * omega_step, omega)
    scale = 1.0 / (length * col_length)

    def lens_of(freqs, gap):
        angle = freqs[:, None, None] * gap[None] * depth_step
        return jnp.stack([jnp.cos(angle) * scale, jnp.sin(angle) * scale])

    def factors(freqs, slow_pair):
        shape = (2, length, LANES)
        return call(
            factor_kernel,
            "factors",
            [SMEM, SMEM, SMEM],
            [shape, shape],
            (freqs, slow_pair, block),
            1 << 27,
            length=length,
            col_length=col_length,
        )

    def columns(value, pair):
        return call(
            columns_kernel,
            "columns",
            [VMEM] * 5,
            [(length, 2 * LANES)],
            (value, *pair, *table_x),
            1 << 30,
        )

    def edges(field, pairs_of, axes):
        parts = field.reshape(8, rows, col_length)
        down = lax.ppermute(parts[:, rows - HALF :], axes, pairs_of(1))
        up = lax.ppermute(parts[:, :HALF], axes, pairs_of(-1))
        return parts, down, up

    padded = [pltpu.VMEM((8, rows + 2 * HALF, col_length), jnp.float32)]
    image_shape = (LAGS, rows, col_length)

    spectra = call(
        rows_kernel,
        "rows",
        [VMEM] * 3,
        [(length, LANES)],
        (fields[0].reshape(flat), *table_y),
        1 << 29,
        rows=rows,
    )
    spectra = exchanged(spectra)
    returned = exchanged(columns(spectra, factors(omega, slow)))
    field, spectra = call(
        turn_kernel,
        "turn",
        [VMEM] * 4 + [SMEM] + [VMEM] * 2,
        [flat, (length, LANES)],
        (
            returned,
            lens_of(omega, lens_gap),
            weight,
            surface.reshape(flat),
            at_end.astype(jnp.int32).reshape(1),
            *table_y,
        ),
        1 << 30,
        rows=rows,
    )

    def along(step):
        return [(i, i + step) for i in range(lane_count) if 0 <= i + step < lane_count]

    spectra = exchanged(spectra)
    parts, above, below = edges(field, along, "lat")
    image = call(
        image_first, "image", [VMEM] * 3, [image_shape], (parts, above, below), 1 << 26, padded, rows=rows
    )
    returned = exchanged(columns(spectra, factors(next_omega, next_slow)))
    field = call(
        end_kernel,
        "end",
        [VMEM] * 5,
        [flat],
        (returned, lens_of(next_omega, next_gap), next_weight, *table_y),
        1 << 30,
        rows=rows,
    )

    def diagonal(step):
        return [
            (s * lane_count + i, (s + 1) % sections * lane_count + i + step)
            for s in range(sections)
            for i in range(lane_count)
            if 0 <= i + step < lane_count
        ]

    parts, above, below = edges(field, diagonal, ("depth", "lat"))
    parts = lax.ppermute(parts, ("depth", "lat"), diagonal(0))
    image = call(
        image_second,
        "image_sum",
        [VMEM] * 4,
        [image_shape],
        (parts, above, below, image),
        1 << 26,
        padded,
        rows=rows,
    )
    return (parts.reshape(fields.shape), image[None, None])


def solution(mesh):
    in_specs = (
        P("depth", None, None, None, "lat", None),
        P(None, None, None, "lat", None),
        P("depth", None),
        P(),
        P("depth", None, None),
        P("depth", None, "lat", None),
        P("depth", None, "lat", None),
        P("depth", None, None),
    )
    out_specs = (P("depth", None, None, None, "lat", None), P("depth", None, None, "lat", None))
    return jax.shard_map(shards, mesh=mesh, in_specs=in_specs, out_specs=out_specs, check_vma=False)
```

profile of v0, /device:TPU:6, one launch (start us, length us, event | category | flops | bytes accessed | tf_op | source)
XLA Modules:
  0.0 119.7 jit_solution(8770456179578602912)
XLA Ops:
  0.6 1.2 %copy-done = bf16[512,1024]{1,0:T(8,128)(2,1)S(1)} copy-done((bf16[512,1024]{1,0:T(8,128)(2,1)S(1)}, bf16[512,1024]{1,0:T(8,128)(2,1)}, u32[]{:S(2)}) %copy-start) | copy-done | bytes 1048600
  1.9 1.2 %copy-done.2 = bf16[512,1024]{1,0:T(8,128)(2,1)S(1)} copy-done((bf16[512,1024]{1,0:T(8,128)(2,1)S(1)}, bf16[512,1024]{1,0:T(8,128)(2,1)}, u32[]{:S(2)}) %copy-start.2) | copy-done | bytes 1048600
  3.1 0.9 copy-done.4
  4.0 1.5 %rows.1 = f32[512,128]{1,0:T(8,128)} custom-call(f32[128,512]{1,0:T(8,128)S(1)} %bitcast.32, bf16[512,1024]{1,0:T(8,128)(2,1)S(1)} %copy-done, bf16[512,1024]{1,0:T(8,128)(2,1)S(1)} %copy-done.2), custom_call_target="tpu_custom_call" | custom-call | flops 536870912 | bytes 1048576 | tf_op jit(solution)/shard_map/rows/pallas_call | solution.py:224
  5.6 11.6 %all-to-all-start = ((f32[32,16,128]{2,1,0:T(8,128)}), f32[32,16,128]{2,1,0:T(8,128)S(1)}, u32[]{:S(2)}, u32[]{:S(2)}) async-start(f32[32,16,128]{2,1,0:T(8,128)} %bitcast.1), calls=%async_computation | async-start | bytes 524288 | tf_op jit(solution)/shard_map/all_to_all | solution.py:238
  17.2 0.6 copy-done.14
  17.8 0.7 copy-done.6
  18.5 1.8 %factors.2 = (f32[2,512,128]{2,1,0:T(8,128)S(1)}, f32[2,512,128]{2,1,0:T(8,128)S(1)}) custom-call(f32[2]{0:T(128)S(1)} %multiply_bitcast_fusion.freq_ref, f32[2]{0:T(128)S(1)} %bitcast.39, s32[1]{0:T(128)} %bitcast.5.block_ref), custom_call_target="tpu_custom_call" | custom-call | flops 134217728 | bytes 1048576 | tf_op jit(solution)/shard_map/factors/pallas_call | solution.py:224
  20.3 0.8 copy-done.10
  21.1 7.3 %all-to-all-done = f32[32,16,128]{2,1,0:T(8,128)S(1)} async-done(((f32[32,16,128]{2,1,0:T(8,128)}), f32[32,16,128]{2,1,0:T(8,128)S(1)}, u32[]{:S(2)}, u32[]{:S(2)}) %all-to-all-start) | async-done | bytes 262176 | tf_op jit(solution)/shard_map/all_to_all | solution.py:238
  28.4 1.0 copy-done.11
  29.4 2.9 %columns.2 = f32[512,256]{1,0:T(8,128)} custom-call(f32[512,128]{1,0:T(8,128)S(1)} %bitcast.36, f32[2,512,128]{2,1,0:T(8,128)S(1)} %get-tuple-element.8.even_ref, f32[2,512,128]{2,1,0:T(8,128)S(1)} %copy-done.11, bf16[512,1024]{1,0:T(8,128)(2,1)S(1)} %copy-done.1, bf16[512,1024]{1,0:T(8,128)(2,1)S(1)} %copy-done.3), custom_call_target="tpu_custom_call" | custom-call | flops 1073741824 | bytes 1048576 | tf_op jit(solution)/shard_map/columns/pallas_call | solution.py:224
  32.3 5.7 %all-to-all-start.1 = ((f32[32,16,256]{2,1,0:T(8,128)}), f32[32,16,256]{2,1,0:T(8,128)S(1)}, u32[]{:S(2)}, u32[]{:S(2)}) async-start(f32[32,16,256]{2,1,0:T(8,128)} %bitcast.6), calls=%async_computation.1 | async-start | bytes 1048576 | tf_op jit(solution)/shard_map/all_to_all | solution.py:238
  38.0 0.6 fusion.7
  38.6 0.7 copy-done.13
  39.2 0.1 select_reduce_fusion
  39.3 0.7 copy-done.5
  40.0 1.3 %add_subtract_fusion = f32[16,512]{1,0:T(8,128)S(1)} fusion(f32[16,512]{1,0:T(8,128)S(1)} %select_reduce_fusion, f32[]{:T(128)} %bitcast.12, f32[]{:T(128)} %bitcast.11, f32[1,1,16,512]{3,2,1,0:T(8,128)S(1)} %copy-done.5), kind=kLoop, calls=%fused_computation.13 | loop fusion | flops 40960 | bytes 98312 | tf_op jit(solution)/shard_map/sub | solution.py:260
  41.2 0.3 fusion
  41.6 12.5 %all-to-all-done.1 = f32[32,16,256]{2,1,0:T(8,128)S(1)} async-done(((f32[32,16,256]{2,1,0:T(8,128)}), f32[32,16,256]{2,1,0:T(8,128)S(1)}, u32[]{:S(2)}, u32[]{:S(2)}) %all-to-all-start.1) | async-done | bytes 524320 | tf_op jit(solution)/shard_map/all_to_all | solution.py:238
  54.0 2.9 %turn.1 = (f32[128,512]{1,0:T(8,128)S(1)}, f32[512,128]{1,0:T(8,128)}) custom-call(f32[512,256]{1,0:T(8,128)S(1)} %bitcast.30, f32[2,2,16,512]{3,2,1,0:T(8,128)S(1)} %pad_maximum_fusion.lens_ref, f32[16,512]{1,0:T(8,128)S(1)} %bitcast.37, f32[128,512]{1,0:T(8,128)S(1)} %bitcast.41, s32[1]{0:T(128)} %bitcast.14.last_ref, bf16[512,1024]{1,0:T(8,128)(2,1)S(1)} %copy-done.1, ...), custom_call_target="tpu_custom_call" | custom-call | flops 1073741824 | bytes 1048576 | tf_op jit(solution)/shard_map/turn/pallas_call | solution.py:224
  56.9 5.6 %all-to-all-start.2 = ((f32[32,16,128]{2,1,0:T(8,128)}), f32[32,16,128]{2,1,0:T(8,128)S(1)}, u32[]{:S(2)}, u32[]{:S(2)}) async-start(f32[32,16,128]{2,1,0:T(8,128)} %bitcast.15), calls=%async_computation.2 | async-start | bytes 524288 | tf_op jit(solution)/shard_map/all_to_all | solution.py:238
  62.5 0.1 broadcast_in_dim.8
  62.6 0.1 reshape.106
  62.6 0.1 pad.4.clone
  62.7 0.1 maximum_maximum_fusion
  62.8 1.0 collective-permute-start
  63.8 2.1 %collective-permute-done = f32[40,512]{1,0:T(8,128)S(1)} collective-permute-done((f32[40,512]{1,0:T(8,128)S(1)}, f32[40,512]{1,0:T(8,128)S(1)}, u32[]{:S(2)}, u32[]{:S(2)}) %collective-permute-start) | collective-permute-done | bytes 81952 | tf_op jit(solution)/shard_map/ppermute | solution.py:263
  65.9 0.1 reduce.slow_ref
  66.0 1.8 %factors.3 = (f32[2,512,128]{2,1,0:T(8,128)S(1)}, f32[2,512,128]{2,1,0:T(8,128)S(1)}) custom-call(f32[2]{0:T(128)S(1)} %broadcast_select_fusion.freq_ref, f32[2]{0:T(128)S(1)} %reduce.slow_ref, s32[1]{0:T(128)} %bitcast.5.block_ref), custom_call_target="tpu_custom_call" | custom-call | flops 134217728 | bytes 1048576 | tf_op jit(solution)/shard_map/factors/pallas_call | solution.py:224
  67.9 0.8 copy-done.8
  68.7 4.3 %all-to-all-done.2 = f32[32,16,128]{2,1,0:T(8,128)S(1)} async-done(((f32[32,16,128]{2,1,0:T(8,128)}), f32[32,16,128]{2,1,0:T(8,128)S(1)}, u32[]{:S(2)}, u32[]{:S(2)}) %all-to-all-start.2) | async-done | bytes 262176 | tf_op jit(solution)/shard_map/all_to_all | solution.py:238
  72.9 1.0 copy-done.9
  74.0 2.9 %columns.3 = f32[512,256]{1,0:T(8,128)} custom-call(f32[512,128]{1,0:T(8,128)S(1)} %bitcast.33, f32[2,512,128]{2,1,0:T(8,128)S(1)} %get-tuple-element.11.even_ref, f32[2,512,128]{2,1,0:T(8,128)S(1)} %copy-done.9, bf16[512,1024]{1,0:T(8,128)(2,1)S(1)} %copy-done.1, bf16[512,1024]{1,0:T(8,128)(2,1)S(1)} %copy-done.3), custom_call_target="tpu_custom_call" | custom-call | flops 1073741824 | bytes 1048576 | tf_op jit(solution)/shard_map/columns/pallas_call | solution.py:224
  76.8 5.7 %all-to-all-start.3 = ((f32[32,16,256]{2,1,0:T(8,128)}), f32[32,16,256]{2,1,0:T(8,128)S(1)}, u32[]{:S(2)}, u32[]{:S(2)}) async-start(f32[32,16,256]{2,1,0:T(8,128)} %bitcast.17), calls=%async_computation.3 | async-start | bytes 1048576 | tf_op jit(solution)/shard_map/all_to_all | solution.py:238
  82.6 0.3 fusion.2
  82.9 0.7 fusion.4
  83.6 3.4 %collective-permute-start.4 = (f32[8,8,512]{2,1,0:T(8,128)}, f32[8,8,512]{2,1,0:T(8,128)S(1)}, u32[]{:S(2)}, u32[]{:S(2)}) collective-permute-start(f32[8,8,512]{2,1,0:T(8,128)} %get-tuple-element.15), channel_id=1, source_target_pairs={{0,1},{1,2},{2,3},{3,4},{4,5},{5,6},{6,7},{7,8},{8,9},{9,10},{10,1... | collective-permute-start | bytes 393224 | tf_op jit(solution)/shard_map/ppermute | solution.py:300
  86.9 2.5 %collective-permute-start.5 = (f32[8,8,512]{2,1,0:T(8,128)S(1)}, f32[8,8,512]{2,1,0:T(8,128)S(1)}, u32[]{:S(2)}, u32[]{:S(2)}) collective-permute-start(f32[8,8,512]{2,1,0:T(8,128)S(1)} %get-tuple-element.14), channel_id=1, source_target_pairs={{1,0},{2,1},{3,2},{4,3},{5,4},{6,5},{7,6},{8,7},{9,8},{10,9},{11,1... | collective-permute-start | bytes 393224 | tf_op jit(solution)/shard_map/ppermute | solution.py:301
  89.4 11.0 %all-to-all-done.3 = f32[32,16,256]{2,1,0:T(8,128)S(1)} async-done(((f32[32,16,256]{2,1,0:T(8,128)}), f32[32,16,256]{2,1,0:T(8,128)S(1)}, u32[]{:S(2)}, u32[]{:S(2)}) %all-to-all-start.3) | async-done | bytes 524320 | tf_op jit(solution)/shard_map/all_to_all | solution.py:238
  100.4 1.4 %end.1 = f32[128,512]{1,0:T(8,128)S(1)} custom-call(f32[512,256]{1,0:T(8,128)S(1)} %bitcast.31, f32[2,2,16,512]{3,2,1,0:T(8,128)S(1)} %pad_maximum_fusion.1.lens_ref, f32[16,512]{1,0:T(8,128)S(1)} %get-tuple-element.18.weight_ref, bf16[512,1024]{1,0:T(8,128)(2,1)S(1)} %copy-done.1, bf16[512,1024]{1,0:T(8,128)(2,1)S(1)} %copy-done.3), custom_call_target="tpu_custom_call" | custom-call | flops 1073741824 | bytes 1048576 | tf_op jit(solution)/shard_map/end/pallas_call | solution.py:224
  101.9 4.9 %collective-permute-start.2 = (f32[8,8,512]{2,1,0:T(8,128)S(1)}, f32[8,8,512]{2,1,0:T(8,128)S(1)}, u32[]{:S(2)}, u32[]{:S(2)}) collective-permute-start(f32[8,8,512]{2,1,0:T(8,128)S(1)} %get-tuple-element.17), channel_id=1, source_target_pairs={{0,33},{1,34},{2,35},{3,36},{4,37},{5,38},{6,39},{7,40},{8,41},{9,... | collective-permute-start | bytes 393224 | tf_op jit(solution)/shard_map/ppermute | solution.py:300
  106.7 1.9 %collective-permute-start.3 = (f32[8,8,512]{2,1,0:T(8,128)S(1)}, f32[8,8,512]{2,1,0:T(8,128)S(1)}, u32[]{:S(2)}, u32[]{:S(2)}) collective-permute-start(f32[8,8,512]{2,1,0:T(8,128)S(1)} %get-tuple-element.16), channel_id=1, source_target_pairs={{1,32},{2,33},{3,34},{4,35},{5,36},{6,37},{7,38},{8,39},{9,40},{10... | collective-permute-start | bytes 393224 | tf_op jit(solution)/shard_map/ppermute | solution.py:301
  108.7 0.4 image.1.base_ref
  109.1 1.7 %collective-permute-done.2.above_ref = f32[8,8,512]{2,1,0:T(8,128)S(1)} collective-permute-done((f32[8,8,512]{2,1,0:T(8,128)S(1)}, f32[8,8,512]{2,1,0:T(8,128)S(1)}, u32[]{:S(2)}, u32[]{:S(2)}) %collective-permute-start.2) | collective-permute-done | bytes 131104 | tf_op jit(solution)/shard_map/ppermute | solution.py:300
  110.8 6.9 %collective-permute-done.3.below_ref = f32[8,8,512]{2,1,0:T(8,128)S(1)} collective-permute-done((f32[8,8,512]{2,1,0:T(8,128)S(1)}, f32[8,8,512]{2,1,0:T(8,128)S(1)}, u32[]{:S(2)}, u32[]{:S(2)}) %collective-permute-start.3) | collective-permute-done | bytes 131104 | tf_op jit(solution)/shard_map/ppermute | solution.py:301
  117.7 1.3 %image_sum.1 = f32[16,16,512]{2,1,0:T(8,128)} custom-call(f32[8,16,512]{2,1,0:T(8,128)S(1)} %collective-permute-done.1.field_ref, f32[8,8,512]{2,1,0:T(8,128)S(1)} %collective-permute-done.2.above_ref, f32[8,8,512]{2,1,0:T(8,128)S(1)} %collective-permute-done.3.below_ref, f32[16,16,512]{2,1,0:T(8,128)S(1)} %image.1.base_ref), custom_call_target="tpu_custom_call" | custom-call | flops 67108864 | bytes 1048576 | tf_op jit(solution)/shard_map/image_sum/pallas_call | solution.py:224
  119.0 0.7 copy.13
  (32 shorter events, 0.1 us)
Async XLA Ops:
  0.6 1.2 %copy-start = (bf16[512,1024]{1,0:T(8,128)(2,1)S(1)}, bf16[512,1024]{1,0:T(8,128)(2,1)}, u32[]{:S(2)}) copy-start(bf16[512,1024]{1,0:T(8,128)(2,1)} %constant.24.clone.lead_ref) | copy-start | bytes 3145732
  1.9 1.2 %copy-start.2 = (bf16[512,1024]{1,0:T(8,128)(2,1)S(1)}, bf16[512,1024]{1,0:T(8,128)(2,1)}, u32[]{:S(2)}) copy-start(bf16[512,1024]{1,0:T(8,128)(2,1)} %constant.25.clone.trail_ref) | copy-start | bytes 3145732
  3.1 0.9 copy-start.4
  4.0 24.3 %copy-start.1 = (bf16[512,1024]{1,0:T(8,128)(2,1)S(1)}, bf16[512,1024]{1,0:T(8,128)(2,1)}, u32[]{:S(2)}) copy-start(bf16[512,1024]{1,0:T(8,128)(2,1)} %constant.24.clone.lead_ref) | copy-start | bytes 3145732
  4.0 24.3 %copy-start.3 = (bf16[512,1024]{1,0:T(8,128)(2,1)S(1)}, bf16[512,1024]{1,0:T(8,128)(2,1)}, u32[]{:S(2)}) copy-start(bf16[512,1024]{1,0:T(8,128)(2,1)} %constant.25.clone.trail_ref) | copy-start | bytes 3145732
  5.6 22.8 %all-to-all-start = ((f32[32,16,128]{2,1,0:T(8,128)}), f32[32,16,128]{2,1,0:T(8,128)S(1)}, u32[]{:S(2)}, u32[]{:S(2)}) async-start(f32[32,16,128]{2,1,0:T(8,128)} %bitcast.1), calls=%async_computation | async-start | bytes 524288 | tf_op jit(solution)/shard_map/all_to_all | solution.py:238
  17.1 0.7 copy-start.14
  17.8 0.7 copy-start.6
  20.3 0.8 copy-start.10
  28.4 1.0 copy-start.11
  32.3 6.3 %copy-start.12 = (s32[1,1,16,512]{3,2,1,0:T(8,128)S(1)}, s32[1,1,16,512]{3,2,1,0:T(8,128)}, u32[]{:S(2)}) copy-start(s32[1,1,16,512]{3,2,1,0:T(8,128)} %param.16) | copy-start | bytes 98308
  32.3 21.7 %all-to-all-start.1 = ((f32[32,16,256]{2,1,0:T(8,128)}), f32[32,16,256]{2,1,0:T(8,128)S(1)}, u32[]{:S(2)}, u32[]{:S(2)}) async-start(f32[32,16,256]{2,1,0:T(8,128)} %bitcast.6), calls=%async_computation.1 | async-start | bytes 1048576 | tf_op jit(solution)/shard_map/all_to_all | solution.py:238
  38.6 0.7 copy-start.13
  39.2 0.8 copy-start.5
  40.0 14.1 %copy-start.7 = (f32[2,2,2,16,512]{4,3,2,1,0:T(8,128)S(1)}, f32[2,2,2,16,512]{4,3,2,1,0:T(8,128)}, u32[]{:S(2)}) copy-start(f32[2,2,2,16,512]{4,3,2,1,0:T(8,128)} %param.11) | copy-start | bytes 786436
  56.9 16.0 %all-to-all-start.2 = ((f32[32,16,128]{2,1,0:T(8,128)}), f32[32,16,128]{2,1,0:T(8,128)S(1)}, u32[]{:S(2)}, u32[]{:S(2)}) async-start(f32[32,16,128]{2,1,0:T(8,128)} %bitcast.15), calls=%async_computation.2 | async-start | bytes 524288 | tf_op jit(solution)/shard_map/all_to_all | solution.py:238
  62.7 1.1 copy-start.15
  62.8 3.1 %collective-permute-start = (f32[40,512]{1,0:T(8,128)S(1)}, f32[40,512]{1,0:T(8,128)S(1)}, u32[]{:S(2)}, u32[]{:S(2)}) collective-permute-start(f32[40,512]{1,0:T(8,128)S(1)} %maximum_maximum_fusion), channel_id=1, source_target_pairs={{0,224},{32,0},{64,32},{96,64},{128,96},{160,128},{192,160},{224,1... | collective-permute-start | bytes 245768 | tf_op jit(solution)/shard_map/ppermute | solution.py:263
  67.9 0.8 copy-start.8
  72.9 1.0 copy-start.9
  76.8 23.6 %all-to-all-start.3 = ((f32[32,16,256]{2,1,0:T(8,128)}), f32[32,16,256]{2,1,0:T(8,128)S(1)}, u32[]{:S(2)}, u32[]{:S(2)}) async-start(f32[32,16,256]{2,1,0:T(8,128)} %bitcast.17), calls=%async_computation.3 | async-start | bytes 1048576 | tf_op jit(solution)/shard_map/all_to_all | solution.py:238
  83.6 25.1 %collective-permute-start.4 = (f32[8,8,512]{2,1,0:T(8,128)}, f32[8,8,512]{2,1,0:T(8,128)S(1)}, u32[]{:S(2)}, u32[]{:S(2)}) collective-permute-start(f32[8,8,512]{2,1,0:T(8,128)} %get-tuple-element.15), channel_id=1, source_target_pairs={{0,1},{1,2},{2,3},{3,4},{4,5},{5,6},{6,7},{7,8},{8,9},{9,10},{10,1... | collective-permute-start | bytes 393224 | tf_op jit(solution)/shard_map/ppermute | solution.py:300
  86.9 21.7 %collective-permute-start.5 = (f32[8,8,512]{2,1,0:T(8,128)S(1)}, f32[8,8,512]{2,1,0:T(8,128)S(1)}, u32[]{:S(2)}, u32[]{:S(2)}) collective-permute-start(f32[8,8,512]{2,1,0:T(8,128)S(1)} %get-tuple-element.14), channel_id=1, source_target_pairs={{1,0},{2,1},{3,2},{4,3},{5,4},{6,5},{7,6},{8,7},{9,8},{10,9},{11,1... | collective-permute-start | bytes 393224 | tf_op jit(solution)/shard_map/ppermute | solution.py:301
  101.8 7.3 %collective-permute-start.1 = (f32[8,16,512]{2,1,0:T(8,128)S(1)}, f32[8,16,512]{2,1,0:T(8,128)S(1)}, u32[]{:S(2)}, u32[]{:S(2)}) collective-permute-start(f32[8,16,512]{2,1,0:T(8,128)S(1)} %bitcast.34), channel_id=1, source_target_pairs={{0,32},{1,33},{2,34},{3,35},{4,36},{5,37},{6,38},{7,39},{8,40},{9,... | collective-permute-start | bytes 786440 | tf_op jit(solution)/shard_map/ppermute | solution.py:363
  101.9 9.0 %collective-permute-start.2 = (f32[8,8,512]{2,1,0:T(8,128)S(1)}, f32[8,8,512]{2,1,0:T(8,128)S(1)}, u32[]{:S(2)}, u32[]{:S(2)}) collective-permute-start(f32[8,8,512]{2,1,0:T(8,128)S(1)} %get-tuple-element.17), channel_id=1, source_target_pairs={{0,33},{1,34},{2,35},{3,36},{4,37},{5,38},{6,39},{7,40},{8,41},{9,... | collective-permute-start | bytes 393224 | tf_op jit(solution)/shard_map/ppermute | solution.py:300
  106.7 10.9 %collective-permute-start.3 = (f32[8,8,512]{2,1,0:T(8,128)S(1)}, f32[8,8,512]{2,1,0:T(8,128)S(1)}, u32[]{:S(2)}, u32[]{:S(2)}) collective-permute-start(f32[8,8,512]{2,1,0:T(8,128)S(1)} %get-tuple-element.16), channel_id=1, source_target_pairs={{1,32},{2,33},{3,34},{4,35},{5,36},{6,37},{7,38},{8,39},{9,40},{10... | collective-permute-start | bytes 393224 | tf_op jit(solution)/shard_map/ppermute | solution.py:301
where the time goes:
time: 121 us; the launch traced here: 120 us
  waiting for transfers between devices  45.7 us (38%)
  starting transfers between devices  42.1 us (35%)
  Pallas kernels  16.8 us (14%)
  local copies, waits for them, and re-layouts  11.9 us (10%)
  other arithmetic  2.2 us (2%)
    all_to_all x4, waiting for transfers between devices, exchanged(): return lax.all_to_all(value, 'lat', split_axis=0, concat_axis=0, tiled=True)  35 us
    all_to_all x4, starting transfers between devices, exchanged(): return lax.all_to_all(value, 'lat', split_axis=0, concat_axis=0, tiled=True)  28.5 us
    pallas_call x9, Pallas kernels, call(): pl.pallas_call(functools.partial(kernel, **params), name=name, in_specs=i...  16.8 us
    unnamed x33, local copies, waits for them, and re-layouts  10.4 us
    ppermute x2, starting transfers between devices, edges(): down = lax.ppermute(parts[:, rows - HALF:], axes, pairs_of(1))  8.23 us
    ppermute x2, waiting for transfers between devices, edges(): up = lax.ppermute(parts[:, :HALF], axes, pairs_of(-1))  6.86 us
    ppermute x2, starting transfers between devices, edges(): up = lax.ppermute(parts[:, :HALF], axes, pairs_of(-1))  4.39 us
  transfers between devices with their start and end apart: 10, of which 7 were waited for; matrix products, arithmetic and copies ran while one was open for 3% of the time, Pallas kernels for 5%

commit v1 on v0

v1 whole, which is shorter than its diff:
```python
import functools
import math

import jax
import jax.numpy as jnp
import ml_dtypes
import numpy as np
from jax import lax
from jax.experimental import pallas as pl
from jax.experimental.pallas import tpu as pltpu
from jax.sharding import PartitionSpec as P

LAGS = 16
HALF = LAGS // 2
REGIONS = 8
GROUPS = 4
CHUNK = 64
LANES = 128
INTERPRET = False

omega_step = 0.04
depth_step = 1.0

COS_TERMS = [(-1.0) ** n / math.factorial(2 * n) for n in range(12)]
SIN_TERMS = [(-1.0) ** n / math.factorial(2 * n + 1) for n in range(12)]


def polynomial(value, terms):
    total = jnp.full_like(value, terms[-1])
    for term in terms[-2::-1]:
        total = total * value + term
    return total


def transform_tables(length):
    half = length // 2
    index = np.arange(half)
    even = 2.0 * np.pi * (2 * index[:, None] * index[None, :] % length) / length
    odd = 2.0 * np.pi * (index[:, None] * (2 * index[None, :] + 1) % length) / length
    tables = []
    for angles in ([even, odd], [odd.T]):
        table = np.concatenate([f(a) for a in angles for f in (np.cos, np.sin)], axis=1)
        lead = table.astype(ml_dtypes.bfloat16)
        trail = (table - lead.astype(np.float64)).astype(ml_dtypes.bfloat16)
        tables.append(jnp.asarray(np.concatenate([lead, trail], axis=1)))
    return tables


class Table:
    def __init__(self, main_ref, odd_ref=None):
        self.main, self.odd = main_ref, odd_ref
        self.width = main_ref.shape[0]

    def part(self, part, first, count, trail):
        if part == 1 and self.odd is not None:
            start = (2 * trail + first) * self.width
            return self.odd[:, start : start + count * self.width]
        start = (4 * trail + 2 * part + first) * self.width
        return self.main[:, start : start + count * self.width]


def two_parts(value):
    lead = value.astype(jnp.bfloat16)
    return lead, (value - lead.astype(jnp.float32)).astype(jnp.bfloat16)


def dot(left, right):
    return jnp.dot(left, right, preferred_element_type=jnp.float32)


def dot_right(value, table, part):
    width = value.shape[1]
    lead, trail = two_parts(value)
    main, rest = table.part(part, 0, 2, 0), table.part(part, 0, 2, 1)
    both = dot(lead, main) + (dot(trail, main) + dot(lead, rest))
    return both[:, :width], both[:, width:]


def dot_left(table, part, value):
    lead, trail = two_parts(value)
    results = []
    for which in range(2):
        main, rest = table.part(part, which, 1, 0), table.part(part, which, 1, 1)
        results.append(dot(main, lead) + (dot(main, trail) + dot(rest, lead)))
    return results


def joined(pairs, axis):
    return [jnp.concatenate([pair[i] for pair in pairs], axis=axis) for i in range(2)]


def analysed_right(value, table):
    half = value.shape[1] // 2
    low, high = value[:, :half], value[:, half:]
    return joined([dot_right(low + high, table, 0), dot_right(low - high, table, 1)], 1)


def restored_right(value, table):
    half = value.shape[1] // 2
    even, odd = dot_right(value[:, :half], table, 0), dot_right(value[:, half:], table, 1)
    return joined([[e + o for e, o in zip(even, odd)], [e - o for e, o in zip(even, odd)]], 1)


def analysed_left(table, value):
    half = value.shape[0] // 2
    low, high = value[:half], value[half:]
    return joined([dot_left(table, 0, low + high), dot_left(table, 1, low - high)], 0)


def restored_left(table, value):
    half = value.shape[0] // 2
    even, odd = dot_left(table, 0, value[:half]), dot_left(table, 1, value[half:])
    return joined([[e + o for e, o in zip(even, odd)], [e - o for e, o in zip(even, odd)]], 0)


def swap_halves(first, second):
    lane = lax.broadcasted_iota(jnp.int32, first.shape, 1)
    low = lane < CHUNK
    return (
        jnp.where(low, first, pltpu.roll(second, CHUNK, 1)),
        jnp.where(low, pltpu.roll(first, CHUNK, 1), second),
    )


def wave_index(position, length):
    half = length // 2
    index = jnp.where(position < half, 2 * position, 2 * (position - half) + 1)
    return jnp.where(index < half, index, index - length).astype(jnp.float32)


def block_row(index, rows):
    return pl.multiple_of(index * rows, rows)


def my_group():
    lat = lax.axis_index("lat")
    members = lax.axis_size("lat") // GROUPS
    return lax.div(lat, members), lax.rem(lat, members)


def omega_pair(held_ref, surface_ref, tick):
    pair = []
    for freq in range(2):
        number = held_ref[freq]
        if tick == 1:
            at_end = lax.axis_index("depth") == lax.axis_size("depth") - 1
            number = jnp.where(at_end, surface_ref[freq], number)
        pair.append(number.astype(jnp.float32) * omega_step)
    return pair


def my_omega(held_ref, surface_ref, tick):
    pair = omega_pair(held_ref, surface_ref, tick)
    return jnp.where(lax.rem(my_group()[0], 2) == 0, pair[0], pair[1])


def lens(angle, scale):
    square = angle * angle
    return (
        polynomial(square, COS_TERMS) * scale,
        angle * polynomial(square, SIN_TERMS) * scale,
    )


def prepare_kernel(
    regions_ref, region_slow_ref, weights_ref, slow_ref, packed_ref, params_ref, *, rows
):
    regions, weight = regions_ref[...], weights_ref[...]
    cell = jnp.full(weight.shape, region_slow_ref[0])
    for region in range(1, REGIONS):
        cell = jnp.where(regions == region, region_slow_ref[region], cell)
    gap = cell - (weight * slow_ref[0] + (1.0 - weight) * slow_ref[1])
    for out in (packed_ref, params_ref):
        out[pl.ds(0, rows), :] = gap
        out[pl.ds(rows, rows), :] = weight
    for ref in range(2):
        params_ref[pl.ds(2 * rows + 8 * ref, 8), :] = jnp.full((8, weight.shape[1]), slow_ref[ref])


def gather_kernel(held_ref, *refs, rows):
    pieces, (weight_ref, lens_ref) = refs[:GROUPS], refs[GROUPS:]
    group = my_group()[0]
    omega = my_omega(held_ref, None, 0)
    sign = jnp.where(group < 2, -1.0, 1.0)
    scale = 1.0 / (weight_ref.shape[1] * (lax.axis_size("lat") * rows))
    for shift in range(GROUPS):
        piece = pieces[shift]
        source = lax.rem(group - shift + GROUPS, GROUPS)
        at = block_row(source, rows)
        weight_ref[pl.ds(at, rows), :] = piece[pl.ds(rows, rows), :]
        cos_part, sin_part = lens(piece[pl.ds(0, rows), :] * omega * depth_step, scale)
        lens_ref[0, pl.ds(at, rows), :] = cos_part
        lens_ref[1, pl.ds(at, rows), :] = sin_part * sign


def lens_kernel(held_ref, surface_freq_ref, passed_ref, lens_ref, *, rows):
    scale = 1.0 / (passed_ref.shape[1] * (lax.axis_size("lat") * rows))
    for freq, omega in enumerate(omega_pair(held_ref, surface_freq_ref, 1)):
        cos_part, sin_part = lens(passed_ref[pl.ds(0, rows), :] * omega * depth_step, scale)
        lens_ref[0, freq] = cos_part
        lens_ref[1, freq] = sin_part


def rows_kernel(field_ref, surface_ref, table_ref, out_ref, *, rows):
    half = field_ref.shape[0] // 2
    members = field_ref.shape[1] // CHUNK
    value = jnp.concatenate([field_ref[...], surface_ref[...]], axis=0)
    cos_part, sin_part = analysed_right(value, Table(table_ref))
    for batch in range(2):
        at_real = 2 * half * batch
        at_imag = at_real + half
        real = cos_part[at_real:at_imag] + sin_part[at_imag : at_imag + half]
        imag = cos_part[at_imag : at_imag + half] - sin_part[at_real:at_imag]
        out_lanes = slice(batch * LANES, (batch + 1) * LANES)
        for tile in range(field_ref.shape[1] // LANES):
            lanes = slice(tile * LANES, (tile + 1) * LANES)
            for at, block in enumerate(swap_halves(real[:, lanes], imag[:, lanes])):
                for group in range(GROUPS):
                    start = (group * members + 2 * tile + at) * rows
                    out_ref[pl.ds(start, rows), out_lanes] = block[group * rows : (group + 1) * rows]


def factor_kernel(held_ref, surface_ref, params_ref, even_ref, odd_ref, *, tick, length, rows):
    col_length = params_ref.shape[1]
    shape = (length, LANES)
    lane = lax.broadcasted_iota(jnp.int32, (1, LANES), 1)
    group, member = my_group()
    wave_y = wave_index(member * CHUNK + lax.rem(lane, CHUNK), col_length) * (
        2.0 * math.pi / col_length
    )
    row = lax.broadcasted_iota(jnp.int32, shape, 0)
    wave_x = wave_index(row, length) * (2.0 * math.pi / length)
    squared = wave_x * wave_x + wave_y * wave_y
    sign = jnp.where(group < 2, -1.0, 1.0)
    first = params_ref[2 * rows : 2 * rows + 1, 0:LANES]
    second = params_ref[2 * rows + 8 : 2 * rows + 9, 0:LANES]
    base = my_omega(held_ref, surface_ref, tick) * jnp.where(lane < CHUNK, first, second)
    gap = base * base - squared
    fade = jnp.exp(-jnp.sqrt(jnp.maximum(-gap, 0.0)) * depth_step)
    inside = jnp.maximum(gap, 0.0)
    even_ref[...] = fade * polynomial(inside, COS_TERMS)
    odd_ref[...] = sign * (fade * (jnp.sqrt(inside) * polynomial(inside, SIN_TERMS)))


def columns_kernel(*refs, rows, tick):
    in_ref, even_ref, odd_ref, table_ref, flip_ref = refs[:5]
    out_ref = refs[-1]
    table, flipped = Table(table_ref), Table(table_ref, flip_ref)
    length = in_ref.shape[0]
    members = length // rows // GROUPS
    order = [(block % members) * GROUPS + block // members for block in range(length // rows)]
    lane = lax.broadcasted_iota(jnp.int32, (length, LANES), 1)
    low = lane < CHUNK
    turn = jnp.where(low, 1.0, -1.0)
    if tick == 0:
        value = in_ref[:, 0:LANES]
    else:
        value = jnp.concatenate([in_ref[pl.ds(at * rows, rows), :] for at in order], axis=0)
        at_end = lax.axis_index("depth") == lax.axis_size("depth") - 1
        value = jnp.where(at_end, refs[5][:, LANES:], value)
    cos_part, sin_part = analysed_left(flipped, value)
    spectrum = cos_part + turn * pltpu.roll(sin_part, CHUNK, 1)
    swapped = pltpu.roll(spectrum, CHUNK, 1)
    even, odd = even_ref[...], odd_ref[...]
    even_turned, odd_turned = pltpu.roll(even, CHUNK, 1), pltpu.roll(odd, CHUNK, 1)
    shifted = [
        spectrum * jnp.where(low, even, even_turned)
        + swapped * jnp.where(low, -odd, odd_turned),
        spectrum * jnp.where(low, even_turned, even)
        + swapped * jnp.where(low, -odd_turned, odd),
    ]
    cos_part, sin_part = restored_left(table, jnp.concatenate(shifted, axis=1))
    for ref in range(2):
        lanes = slice(ref * LANES, (ref + 1) * LANES)
        result = cos_part[:, lanes] - turn * pltpu.roll(sin_part[:, lanes], CHUNK, 1)
        if tick == 1:
            out_ref[:, lanes] = result
        else:
            for block, at in enumerate(order):
                out_ref[pl.ds(at * rows, rows), lanes] = result[block * rows : (block + 1) * rows]


def inverse_rows(in_ref, table, groups, rows):
    length = in_ref.shape[0] // (groups * rows) * CHUNK
    members = length // CHUNK
    stacked = []
    for ref in range(2):
        lanes = slice(ref * LANES, (ref + 1) * LANES)
        for group in range(groups):
            tiles = []
            for tile in range(length // LANES):
                first = (group * members + 2 * tile) * rows
                tiles.append(
                    swap_halves(
                        in_ref[pl.ds(first, rows), lanes], in_ref[pl.ds(first + rows, rows), lanes]
                    )
                )
            stacked += joined(tiles, 1)
    cos_part, sin_part = restored_right(jnp.concatenate(stacked, axis=0), table)
    results = []
    for ref in range(2):
        for group in range(groups):
            at = (ref * groups + group) * 2 * rows
            real, imag = slice(at, at + rows), slice(at + rows, at + 2 * rows)
            results.append((cos_part[real] - sin_part[imag], cos_part[imag] + sin_part[real]))
    return results[:groups], results[groups:]


def lensed(first, second, weight, lens_cos, lens_sin):
    real = weight * first[0] + (1.0 - weight) * second[0]
    imag = weight * first[1] + (1.0 - weight) * second[1]
    return real * lens_cos - imag * lens_sin, real * lens_sin + imag * lens_cos


def turn_kernel(in_ref, weight_ref, lens_ref, table_ref, flip_ref, *refs, rows):
    out_ref, pieces, field_ref = refs[0], refs[1:5], refs[5]
    held = GROUPS * rows
    first, second = inverse_rows(in_ref, Table(table_ref, flip_ref), 1, held)
    field = lensed(first[0], second[0], weight_ref[...], lens_ref[0], lens_ref[1])
    for part in range(2):
        field_ref[part] = field[part]
    group = my_group()[0]
    for shift in range(GROUPS):
        at = block_row(lax.rem(group + shift, GROUPS), rows)
        for part in range(2):
            pieces[shift][part] = field_ref[part, pl.ds(at, rows), :]
    cos_part, sin_part = analysed_right(jnp.concatenate(field, axis=0), Table(table_ref))
    real, imag = cos_part[:held] + sin_part[held:], cos_part[held:] - sin_part[:held]
    for tile in range(real.shape[1] // LANES):
        lanes = slice(tile * LANES, (tile + 1) * LANES)
        for at, block in enumerate(swap_halves(real[:, lanes], imag[:, lanes])):
            out_ref[pl.ds((2 * tile + at) * held, held), :] = block


def assemble_kernel(*refs, rows):
    pieces, (parts_ref, tail_ref, head_ref) = refs[:GROUPS], refs[GROUPS:]
    group = my_group()[0]
    for shift in range(GROUPS):
        source = lax.rem(group - shift + GROUPS, GROUPS)
        for part in range(2):
            value = pieces[shift][part]
            parts_ref[part * GROUPS + source] = value
            tail_ref[part * GROUPS + source] = value[rows - HALF :]
            head_ref[part * GROUPS + source] = value[:HALF]


def end_kernel(in_ref, lens_ref, params_ref, table_ref, flip_ref, *out_refs, rows):
    parts_ref, tail_ref, head_ref = out_refs
    first, second = inverse_rows(in_ref, Table(table_ref, flip_ref), GROUPS, rows)
    weight = params_ref[pl.ds(rows, rows), :]
    for group in range(GROUPS):
        lens_sin = lens_ref[1, group % 2]
        field = lensed(
            first[group],
            second[group],
            weight,
            lens_ref[0, group % 2],
            lens_sin if group >= 2 else -lens_sin,
        )
        for part in range(2):
            parts_ref[part * GROUPS + group] = field[part]
            tail_ref[part * GROUPS + group] = field[part][rows - HALF :]
            head_ref[part * GROUPS + group] = field[part][:HALF]


def image_body(field_ref, above_ref, below_ref, base_ref, out_ref, padded_ref, rows):
    for index in range(8):
        padded_ref[index, pl.ds(0, HALF)] = above_ref[index]
        padded_ref[index, pl.ds(HALF, rows)] = field_ref[index]
        padded_ref[index, pl.ds(HALF + rows, HALF)] = below_ref[index]
    for lag in range(LAGS):
        offset = lag - HALF
        total = None if base_ref is None else base_ref[lag]
        for part in range(2):
            for freq in range(2):
                source = padded_ref[part * 4 + freq, pl.ds(HALF - offset, rows)]
                receiver = padded_ref[part * 4 + 2 + freq, pl.ds(HALF + offset, rows)]
                total = source * receiver if total is None else total + source * receiver
        out_ref[lag] = total


def image_first(field_ref, above_ref, below_ref, out_ref, padded_ref, *, rows):
    image_body(field_ref, above_ref, below_ref, None, out_ref, padded_ref, rows)


def image_second(field_ref, above_ref, below_ref, base_ref, out_ref, padded_ref, *, rows):
    image_body(field_ref, above_ref, below_ref, base_ref, out_ref, padded_ref, rows)


VMEM = pl.BlockSpec(memory_space=pltpu.VMEM)
SMEM = pl.BlockSpec(memory_space=pltpu.SMEM)


def call(kernel, in_specs, out_shapes, operands, flops, scratch=(), **params):
    many = len(out_shapes) > 1
    shapes = [jax.ShapeDtypeStruct(shape, jnp.float32) for shape in out_shapes]
    return pl.pallas_call(
        functools.partial(kernel, **params),
        in_specs=in_specs,
        out_specs=[VMEM] * len(shapes) if many else VMEM,
        out_shape=shapes if many else shapes[0],
        scratch_shapes=list(scratch),
        cost_estimate=pl.CostEstimate(flops=flops, bytes_accessed=1 << 20, transcendentals=0),
        compiler_params=pltpu.CompilerParams(vmem_limit_bytes=24 << 20),
        interpret=INTERPRET,
    )(*operands)


def shards(
    fields, surface, held_freqs, surface_freqs, ref_slowness, weights, regions, region_slowness
):
    lane_count = lax.axis_size("lat")
    sections = lax.axis_size("depth")
    rows, col_length = fields.shape[4], fields.shape[5]
    length = lane_count * rows
    members = lane_count // GROUPS
    held = GROUPS * rows
    tables_y = transform_tables(col_length)
    tables_x = tables_y if length == col_length else transform_tables(length)
    groups = [[group * members + i for i in range(members)] for group in range(GROUPS)]
    held_freqs = held_freqs[0]

    def exchanged(value, within=None):
        return lax.all_to_all(
            value, "lat", split_axis=0, concat_axis=0, tiled=True, axis_index_groups=within
        )

    def across(pieces):
        moved = [pieces[0]]
        for shift in range(1, GROUPS):
            pairs = [(i, (i + shift * members) % lane_count) for i in range(lane_count)]
            moved.append(lax.ppermute(pieces[shift], "lat", pairs))
        return moved

    def factors(params, tick):
        shape = (length, LANES)
        return call(
            factor_kernel,
            [SMEM, SMEM, VMEM],
            [shape, shape],
            (held_freqs, surface_freqs, params),
            1 << 27,
            tick=tick,
            length=length,
            rows=rows,
        )

    def columns(value, pair, tick, *more):
        return call(
            columns_kernel,
            [VMEM] * (5 + len(more)),
            [(length, 2 * LANES)],
            (value, *pair, *tables_x, *more),
            1 << 29,
            rows=rows,
            tick=tick,
        )

    padded = [pltpu.VMEM((8, rows + 2 * HALF, col_length), jnp.float32)]
    image_shape = (LAGS, rows, col_length)
    parts_shape, edge_shape = (8, rows, col_length), (8, HALF, col_length)
    packed_shape, params_shape = (2 * rows, col_length), (2 * rows + 16, col_length)

    spectra = call(
        rows_kernel,
        [VMEM] * 3,
        [(length, 2 * LANES)],
        (fields.reshape(8 * rows, col_length), surface.reshape(8 * rows, col_length), tables_y[0]),
        1 << 28,
        rows=rows,
    )
    packed, params = call(
        prepare_kernel,
        [VMEM, SMEM, VMEM, SMEM],
        [packed_shape, params_shape],
        (
            regions[0, 0],
            region_slowness[0, 0],
            weights[0, 0],
            ref_slowness[0, 0],
        ),
        1 << 24,
        rows=rows,
    )
    entered = exchanged(spectra)
    packed = across([packed] * GROUPS)
    pair = factors(params, 0)
    shifted = columns(entered, pair, 0)
    returned = exchanged(shifted, groups)
    passed = lax.ppermute(params, "depth", [(s, (s - 1) % sections) for s in range(sections)])
    returned, passed = lax.optimization_barrier((returned, passed))
    weight, lenses = call(
        gather_kernel,
        [SMEM] + [VMEM] * GROUPS,
        [(held, col_length), (2, held, col_length)],
        (held_freqs, *packed),
        1 << 25,
        rows=rows,
    )
    spectra, *pieces = call(
        turn_kernel,
        [VMEM] * 5,
        [(length, LANES)] + [(2, rows, col_length)] * GROUPS,
        (returned, weight, lenses, *tables_y),
        1 << 29,
        [pltpu.VMEM((2, held, col_length), jnp.float32)],
        rows=rows,
    )
    spectra = exchanged(spectra, groups)
    pieces = across(pieces)

    def along(step):
        return [(i, i + step) for i in range(lane_count) if 0 <= i + step < lane_count]

    parts, tail, head = call(
        assemble_kernel,
        [VMEM] * GROUPS,
        [parts_shape, edge_shape, edge_shape],
        pieces,
        1 << 20,
        rows=rows,
    )
    above = lax.ppermute(tail, "lat", along(1))
    below = lax.ppermute(head, "lat", along(-1))
    image = call(
        image_first, [VMEM] * 3, [image_shape], (parts, above, below), 1 << 26, padded, rows=rows
    )
    pair = factors(passed, 1)
    shifted = columns(spectra, pair, 1, entered)
    returned = exchanged(shifted)
    returned, image = lax.optimization_barrier((returned, image))
    lenses = call(
        lens_kernel,
        [SMEM, SMEM, VMEM],
        [(2, 2, rows, col_length)],
        (held_freqs, surface_freqs, passed),
        1 << 24,
        rows=rows,
    )
    parts, tail, head = call(
        end_kernel,
        [VMEM] * 5,
        [parts_shape, edge_shape, edge_shape],
        (returned, lenses, passed, *tables_y),
        1 << 29,
        rows=rows,
    )

    def diagonal(step):
        return [
            (s * lane_count + i, (s + 1) % sections * lane_count + i + step)
            for s in range(sections)
            for i in range(lane_count)
            if 0 <= i + step < lane_count
        ]

    above = lax.ppermute(tail, ("depth", "lat"), diagonal(1))
    below = lax.ppermute(head, ("depth", "lat"), diagonal(-1))
    parts = lax.ppermute(parts, ("depth", "lat"), diagonal(0))
    image = call(
        image_second,
        [VMEM] * 4,
        [image_shape],
        (parts, above, below, image),
        1 << 26,
        padded,
        rows=rows,
    )
    return (parts.reshape(fields.shape), image[None, None])


def solution(mesh):
    in_specs = (
        P("depth", None, None, None, "lat", None),
        P(None, None, None, "lat", None),
        P("depth", None),
        P(),
        P("depth", None, None),
        P("depth", None, "lat", None),
        P("depth", None, "lat", None),
        P("depth", None, None),
    )
    out_specs = (P("depth", None, None, None, "lat", None), P("depth", None, None, "lat", None))

    return jax.shard_map(shards, mesh=mesh, in_specs=in_specs, out_specs=out_specs, check_vma=False)
```

time: 121 us -> 126 us (1.041)
  starting transfers between devices: 42.1 us -> 58.7 us
  local copies, waits for them, and re-layouts: 11.9 us -> 3.86 us
  Pallas kernels: 16.8 us -> 14.2 us
  other arithmetic: 2.2 us -> 0 us
  waiting for transfers between devices: 45.7 us -> 47.2 us
    ppermute x5 -> x11, waiting for transfers between devices: 10.7 us -> 28.7 us  [the longest x6 16.7 us: across(): moved.append(lax.ppermute(pieces[shift], 'lat', pairs))]
    all_to_all x4, waiting for transfers between devices: 35 us -> 18.5 us  [exchanged(): lax.all_to_all(value, 'lat', split_axis=0, concat_axis=0, tiled=True, axi...]
    ppermute x5 -> x11, starting transfers between devices: 13.6 us -> 29.3 us  [the longest x6 15.4 us: across(): moved.append(lax.ppermute(pieces[shift], 'lat', pairs))]
    unnamed x33 -> x23, local copies, waits for them, and re-layouts: 10.4 us -> 3.86 us
    pallas_call x9 -> x13, Pallas kernels: 16.8 us -> 14.2 us  [call(): pl.pallas_call(functools.partial(kernel, **params), in_specs=in_specs, ou...]
    slice x5 -> x0, local copies, waits for them, and re-layouts: 1.3 us -> none  [the longest x2 0.69 us: edges(): up = lax.ppermute(parts[:, :HALF], axes, pairs_of(-1))]
  transfers between devices with their start and end apart: 10 -> 16, of which waited for: 7 -> 10; matrix products, arithmetic and copies ran while one was open for 3% -> 0% of each run, Pallas kernels for 5% -> 4%
where the time goes in v1:
time: 126 us; the launch traced here: 125 us
  starting transfers between devices  58.7 us (47%)
  waiting for transfers between devices  47.2 us (37%)
  Pallas kernels  14.2 us (11%)
  local copies, waits for them, and re-layouts  3.86 us (3%)
    all_to_all x4, starting transfers between devices, exchanged(): lax.all_to_all(value, 'lat', split_axis=0, concat_axis=0, tiled=True, axi...  29.4 us
    all_to_all x4, waiting for transfers between devices, exchanged(): lax.all_to_all(value, 'lat', split_axis=0, concat_axis=0, tiled=True, axi...  18.5 us
    ppermute x6, waiting for transfers between devices, across(): moved.append(lax.ppermute(pieces[shift], 'lat', pairs))  16.7 us
    ppermute x6, starting transfers between devices, across(): moved.append(lax.ppermute(pieces[shift], 'lat', pairs))  15.4 us
    pallas_call x13, Pallas kernels, call(): pl.pallas_call(functools.partial(kernel, **params), in_specs=in_specs, ou...  14.2 us
    ppermute x1, waiting for transfers between devices, shards(): below = lax.ppermute(head, ('depth', 'lat'), diagonal(-1))  5.7 us
    ppermute x1, waiting for transfers between devices, shards(): below = lax.ppermute(head, 'lat', along(-1))  4.56 us
    unnamed x23, local copies, waits for them, and re-layouts  3.86 us
  transfers between devices with their start and end apart: 16, of which 10 were waited for; matrix products, arithmetic and copies ran while one was open for 0% of the time, Pallas kernels for 4%

profile of v1, /device:TPU:6, one launch (start us, length us, event | category | flops | bytes accessed | tf_op | source)
XLA Modules:
  0.0 124.8 jit_solution(17173439493906311908)
XLA Ops:
  0.6 0.0 copy-start
  0.6 1.2 copy-done
  1.9 0.9 copy-done.3
  2.8 0.9 copy-done.4
  3.8 1.5 %shard_map.113 = f32[512,256]{1,0:T(8,128)} custom-call(f32[128,512]{1,0:T(8,128)S(1)} %bitcast.23, f32[128,512]{1,0:T(8,128)S(1)} %bitcast.24, bf16[256,2048]{1,0:T(8,128)(2,1)S(1)} %copy-done), custom_call_target="tpu_custom_call" | custom-call | flops 268435456 | bytes 1048576 | tf_op jit(solution)/shard_map/pallas_call | solution.py:397
  5.3 0.0 copy-start.10
  5.3 11.7 %all-to-all-start = ((f32[32,16,256]{2,1,0:T(8,128)}), f32[32,16,256]{2,1,0:T(8,128)S(1)}, u32[]{:S(2)}, u32[]{:S(2)}) async-start(f32[32,16,256]{2,1,0:T(8,128)} %bitcast.2), calls=%async_computation | async-start | bytes 1048576 | tf_op jit(solution)/shard_map/all_to_all | solution.py:424
  17.0 0.0 copy-start.2
  17.1 0.6 shard_map.114
  17.7 1.2 shard_map.115
  18.9 14.9 %all-to-all-done = f32[32,16,256]{2,1,0:T(8,128)S(1)} async-done(((f32[32,16,256]{2,1,0:T(8,128)}), f32[32,16,256]{2,1,0:T(8,128)S(1)}, u32[]{:S(2)}, u32[]{:S(2)}) %all-to-all-start) | async-done | bytes 524320 | tf_op jit(solution)/shard_map/all_to_all | solution.py:424
  33.8 2.0 %shard_map.116 = f32[512,256]{1,0:T(8,128)} custom-call(f32[512,256]{1,0:T(8,128)S(1)} %bitcast.17, f32[512,128]{1,0:T(8,128)S(1)} %get-tuple-element.26.refs_1_, f32[512,128]{1,0:T(8,128)S(1)} %get-tuple-element.27.refs_2_, bf16[256,2048]{1,0:T(8,128)(2,1)S(1)} %copy-done.1, bf16[256,1024]{1,0:T(8,128)(2,1)S(1)} %copy-done.2), custom_call_target="tpu_custom_call" | custom-call | flops 536870912 | bytes 1048576 | tf_op jit(solution)/shard_map/pallas_call | solution.py:397
  35.9 4.8 %all-to-all-start.1 = ((f32[8,64,256]{2,1,0:T(8,128)}), f32[8,64,256]{2,1,0:T(8,128)S(1)}, u32[]{:S(2)}, u32[]{:S(2)}) async-start(f32[8,64,256]{2,1,0:T(8,128)} %bitcast.9), calls=%async_computation.1 | async-start | bytes 1048576 | tf_op jit(solution)/shard_map/all_to_all | solution.py:424
  40.7 0.5 collective-permute-start
  41.2 1.4 %collective-permute-start.1 = (f32[32,512]{1,0:T(8,128)S(1)}, f32[32,512]{1,0:T(8,128)S(1)}, u32[]{:S(2)}, u32[]{:S(2)}) collective-permute-start(f32[32,512]{1,0:T(8,128)S(1)} %get-tuple-element.29.refs_0_), channel_id=1, source_target_pairs={{0,8},{1,9},{2,10},{3,11},{4,12},{5,13},{6,14},{7,15},{8,16},{9,17... | collective-permute-start | bytes 196616 | tf_op jit(solution)/shard_map/ppermute | solution.py:432
  42.5 2.7 %collective-permute-start.2 = (f32[32,512]{1,0:T(8,128)S(1)}, f32[32,512]{1,0:T(8,128)S(1)}, u32[]{:S(2)}, u32[]{:S(2)}) collective-permute-start(f32[32,512]{1,0:T(8,128)S(1)} %get-tuple-element.29.refs_0_), channel_id=1, source_target_pairs={{0,16},{1,17},{2,18},{3,19},{4,20},{5,21},{6,22},{7,23},{8,24},{9,... | collective-permute-start | bytes 196616 | tf_op jit(solution)/shard_map/ppermute | solution.py:432
  45.2 1.7 %collective-permute-start.3 = (f32[32,512]{1,0:T(8,128)S(1)}, f32[32,512]{1,0:T(8,128)S(1)}, u32[]{:S(2)}, u32[]{:S(2)}) collective-permute-start(f32[32,512]{1,0:T(8,128)S(1)} %get-tuple-element.29.refs_0_), channel_id=1, source_target_pairs={{0,24},{1,25},{2,26},{3,27},{4,28},{5,29},{6,30},{7,31},{8,0},{9,1... | collective-permute-start | bytes 196616 | tf_op jit(solution)/shard_map/ppermute | solution.py:432
  47.0 4.9 %collective-permute-done.1.refs_1_ = f32[32,512]{1,0:T(8,128)S(1)} collective-permute-done((f32[32,512]{1,0:T(8,128)S(1)}, f32[32,512]{1,0:T(8,128)S(1)}, u32[]{:S(2)}, u32[]{:S(2)}) %collective-permute-start.1) | collective-permute-done | bytes 65568 | tf_op jit(solution)/shard_map/ppermute | solution.py:432
  51.8 0.0 collective-permute-done.2.refs_2_
  51.8 1.3 %collective-permute-done.3.refs_3_ = f32[32,512]{1,0:T(8,128)S(1)} collective-permute-done((f32[32,512]{1,0:T(8,128)S(1)}, f32[32,512]{1,0:T(8,128)S(1)}, u32[]{:S(2)}, u32[]{:S(2)}) %collective-permute-start.3) | collective-permute-done | bytes 65568 | tf_op jit(solution)/shard_map/ppermute | solution.py:432
  53.1 0.8 shard_map.117
  53.9 0.0 collective-permute-done.params_ref.passed_ref
  53.9 0.0 all-to-all-done.1
  53.9 1.9 %shard_map.118 = (f32[512,128]{1,0:T(8,128)}, f32[2,16,512]{2,1,0:T(8,128)S(1)}, f32[2,16,512]{2,1,0:T(8,128)S(1)}, f32[2,16,512]{2,1,0:T(8,128)S(1)}, f32[2,16,512]{2,1,0:T(8,128)S(1)}) custom-call(f32[512,256]{1,0:T(8,128)S(1)} %bitcast.19, f32[64,512]{1,0:T(8,128)S(1)} %get-tuple-element.30.weight_ref, f32[2,64,512]{2,1,0:T(8,128)S(1)} %get-tuple-element.31.lens_ref, ...), custom_call_target="tpu_custom_call" | custom-call | flops 536870912 | bytes 1048576 | tf_op jit(solution)/shard_map/pallas_call | solution.py:397
  55.8 5.8 %all-to-all-start.2 = ((f32[8,64,128]{2,1,0:T(8,128)}), f32[8,64,128]{2,1,0:T(8,128)S(1)}, u32[]{:S(2)}, u32[]{:S(2)}) async-start(f32[8,64,128]{2,1,0:T(8,128)} %bitcast.11), calls=%async_computation.2 | async-start | bytes 524288 | tf_op jit(solution)/shard_map/all_to_all | solution.py:424
  61.6 1.2 shard_map.119
  62.8 3.6 %all-to-all-done.2 = f32[8,64,128]{2,1,0:T(8,128)S(1)} async-done(((f32[8,64,128]{2,1,0:T(8,128)}), f32[8,64,128]{2,1,0:T(8,128)S(1)}, u32[]{:S(2)}, u32[]{:S(2)}) %all-to-all-start.2) | async-done | bytes 262176 | tf_op jit(solution)/shard_map/all_to_all | solution.py:424
  66.4 2.0 %shard_map.120 = f32[512,256]{1,0:T(8,128)} custom-call(f32[512,128]{1,0:T(8,128)S(1)} %bitcast.22, f32[512,128]{1,0:T(8,128)S(1)} %get-tuple-element.34.refs_1_, f32[512,128]{1,0:T(8,128)S(1)} %get-tuple-element.35.refs_2_, bf16[256,2048]{1,0:T(8,128)(2,1)S(1)} %copy-done.1, bf16[256,1024]{1,0:T(8,128)(2,1)S(1)} %copy-done.2, f32[512,256]{1,0:T(8,128)S(1)} %bitcast.18), custom_call_target="tpu_custom_call" | custom-call | flops 536870912 | bytes 1048576 | tf_op jit(solution)/shard_map/pallas_call | solution.py:397
  68.4 7.0 %all-to-all-start.3 = ((f32[32,16,256]{2,1,0:T(8,128)}), f32[32,16,256]{2,1,0:T(8,128)S(1)}, u32[]{:S(2)}, u32[]{:S(2)}) async-start(f32[32,16,256]{2,1,0:T(8,128)} %bitcast.13), calls=%async_computation.3 | async-start | bytes 1048576 | tf_op jit(solution)/shard_map/all_to_all | solution.py:424
  75.4 2.4 %collective-permute-start.4 = (f32[2,16,512]{2,1,0:T(8,128)S(1)}, f32[2,16,512]{2,1,0:T(8,128)S(1)}, u32[]{:S(2)}, u32[]{:S(2)}) collective-permute-start(f32[2,16,512]{2,1,0:T(8,128)S(1)} %get-tuple-element.37), channel_id=1, source_target_pairs={{0,8},{1,9},{2,10},{3,11},{4,12},{5,13},{6,14},{7,15},{8,16},{9,17... | collective-permute-start | bytes 196616 | tf_op jit(solution)/shard_map/ppermute | solution.py:432
  77.9 3.6 %collective-permute-start.5 = (f32[2,16,512]{2,1,0:T(8,128)S(1)}, f32[2,16,512]{2,1,0:T(8,128)S(1)}, u32[]{:S(2)}, u32[]{:S(2)}) collective-permute-start(f32[2,16,512]{2,1,0:T(8,128)S(1)} %get-tuple-element.38), channel_id=1, source_target_pairs={{0,16},{1,17},{2,18},{3,19},{4,20},{5,21},{6,22},{7,23},{8,24},{9,... | collective-permute-start | bytes 196616 | tf_op jit(solution)/shard_map/ppermute | solution.py:432
  81.5 3.5 %collective-permute-start.6 = (f32[2,16,512]{2,1,0:T(8,128)S(1)}, f32[2,16,512]{2,1,0:T(8,128)S(1)}, u32[]{:S(2)}, u32[]{:S(2)}) collective-permute-start(f32[2,16,512]{2,1,0:T(8,128)S(1)} %get-tuple-element.39), channel_id=1, source_target_pairs={{0,24},{1,25},{2,26},{3,27},{4,28},{5,29},{6,30},{7,31},{8,0},{9,1... | collective-permute-start | bytes 196616 | tf_op jit(solution)/shard_map/ppermute | solution.py:432
  85.0 8.1 %collective-permute-done.4.refs_1_ = f32[2,16,512]{2,1,0:T(8,128)S(1)} collective-permute-done((f32[2,16,512]{2,1,0:T(8,128)S(1)}, f32[2,16,512]{2,1,0:T(8,128)S(1)}, u32[]{:S(2)}, u32[]{:S(2)}) %collective-permute-start.4) | collective-permute-done | bytes 65568 | tf_op jit(solution)/shard_map/ppermute | solution.py:432
  93.2 2.4 %collective-permute-done.5.refs_2_ = f32[2,16,512]{2,1,0:T(8,128)S(1)} collective-permute-done((f32[2,16,512]{2,1,0:T(8,128)S(1)}, f32[2,16,512]{2,1,0:T(8,128)S(1)}, u32[]{:S(2)}, u32[]{:S(2)}) %collective-permute-start.5) | collective-permute-done | bytes 65568 | tf_op jit(solution)/shard_map/ppermute | solution.py:432
  95.7 2.4 %collective-permute-start.7 = (f32[8,8,512]{2,1,0:T(8,128)S(1)}, f32[8,8,512]{2,1,0:T(8,128)S(1)}, u32[]{:S(2)}, u32[]{:S(2)}) collective-permute-start(f32[8,8,512]{2,1,0:T(8,128)S(1)} %get-tuple-element.41), channel_id=1, source_target_pairs={{0,1},{1,2},{2,3},{3,4},{4,5},{5,6},{6,7},{7,8},{8,9},{9,10},{10,1... | collective-permute-start | bytes 393224 | tf_op jit(solution)/shard_map/ppermute | solution.py:523
  98.1 3.4 %collective-permute-start.8 = (f32[8,8,512]{2,1,0:T(8,128)S(1)}, f32[8,8,512]{2,1,0:T(8,128)S(1)}, u32[]{:S(2)}, u32[]{:S(2)}) collective-permute-start(f32[8,8,512]{2,1,0:T(8,128)S(1)} %get-tuple-element.42), channel_id=1, source_target_pairs={{1,0},{2,1},{3,2},{4,3},{5,4},{6,5},{7,6},{8,7},{9,8},{10,9},{11,1... | collective-permute-start | bytes 393224 | tf_op jit(solution)/shard_map/ppermute | solution.py:524
  101.5 0.7 shard_map.123.lens_ref
  102.2 0.3 collective-permute-done.7.above_ref
  102.5 4.6 %collective-permute-done.8.below_ref = f32[8,8,512]{2,1,0:T(8,128)S(1)} collective-permute-done((f32[8,8,512]{2,1,0:T(8,128)S(1)}, f32[8,8,512]{2,1,0:T(8,128)S(1)}, u32[]{:S(2)}, u32[]{:S(2)}) %collective-permute-start.8) | collective-permute-done | bytes 131104 | tf_op jit(solution)/shard_map/ppermute | solution.py:524
  107.1 0.4 shard_map.122.base_ref
  107.5 0.7 shard_map.124
  108.2 0.0 collective-permute-start.9
  108.2 3.8 %collective-permute-start.10 = (f32[8,8,512]{2,1,0:T(8,128)S(1)}, f32[8,8,512]{2,1,0:T(8,128)S(1)}, u32[]{:S(2)}, u32[]{:S(2)}) collective-permute-start(f32[8,8,512]{2,1,0:T(8,128)S(1)} %get-tuple-element.45), channel_id=1, source_target_pairs={{0,33},{1,34},{2,35},{3,36},{4,37},{5,38},{6,39},{7,40},{8,41},{9,... | collective-permute-start | bytes 393224 | tf_op jit(solution)/shard_map/ppermute | solution.py:557
  112.0 3.8 %collective-permute-start.11 = (f32[8,8,512]{2,1,0:T(8,128)S(1)}, f32[8,8,512]{2,1,0:T(8,128)S(1)}, u32[]{:S(2)}, u32[]{:S(2)}) collective-permute-start(f32[8,8,512]{2,1,0:T(8,128)S(1)} %get-tuple-element.46), channel_id=1, source_target_pairs={{1,32},{2,33},{3,34},{4,35},{5,36},{6,37},{7,38},{8,39},{9,40},{10... | collective-permute-start | bytes 393224 | tf_op jit(solution)/shard_map/ppermute | solution.py:558
  115.8 1.3 %collective-permute-done.10.above_ref = f32[8,8,512]{2,1,0:T(8,128)S(1)} collective-permute-done((f32[8,8,512]{2,1,0:T(8,128)S(1)}, f32[8,8,512]{2,1,0:T(8,128)S(1)}, u32[]{:S(2)}, u32[]{:S(2)}) %collective-permute-start.10) | collective-permute-done | bytes 131104 | tf_op jit(solution)/shard_map/ppermute | solution.py:557
  117.2 5.7 %collective-permute-done.11.below_ref = f32[8,8,512]{2,1,0:T(8,128)S(1)} collective-permute-done((f32[8,8,512]{2,1,0:T(8,128)S(1)}, f32[8,8,512]{2,1,0:T(8,128)S(1)}, u32[]{:S(2)}, u32[]{:S(2)}) %collective-permute-start.11) | collective-permute-done | bytes 131104 | tf_op jit(solution)/shard_map/ppermute | solution.py:558
  122.9 1.3 %shard_map.125 = f32[16,16,512]{2,1,0:T(8,128)} custom-call(f32[8,16,512]{2,1,0:T(8,128)S(1)} %collective-permute-done.9.field_ref, f32[8,8,512]{2,1,0:T(8,128)S(1)} %collective-permute-done.10.above_ref, f32[8,8,512]{2,1,0:T(8,128)S(1)} %collective-permute-done.11.below_ref, f32[16,16,512]{2,1,0:T(8,128)S(1)} %shard_map.122.base_ref), custom_call_target="tpu_custom_call" | custom-call | flops 67108864 | bytes 1048576 | tf_op jit(solution)/shard_map/pallas_call | solution.py:397
  124.1 0.7 copy.13
  (20 shorter events, 0.1 us)
Async XLA Ops:
  0.6 1.2 copy-start
  1.9 0.9 copy-start.3
  2.8 0.9 copy-start.4
  3.8 13.3 %copy-start.5 = (s32[1,1,16,512]{3,2,1,0:T(8,128)S(1)}, s32[1,1,16,512]{3,2,1,0:T(8,128)}, u32[]{:S(2)}) copy-start(s32[1,1,16,512]{3,2,1,0:T(8,128)} %param.16) | copy-start | bytes 98308
  3.8 13.3 %copy-start.6 = (f32[1,1,16,512]{3,2,1,0:T(8,128)S(1)}, f32[1,1,16,512]{3,2,1,0:T(8,128)}, u32[]{:S(2)}) copy-start(f32[1,1,16,512]{3,2,1,0:T(8,128)} %param.15) | copy-start | bytes 98308
  5.3 28.6 %copy-start.1 = (bf16[256,2048]{1,0:T(8,128)(2,1)S(1)}, bf16[256,2048]{1,0:T(8,128)(2,1)}, u32[]{:S(2)}) copy-start(bf16[256,2048]{1,0:T(8,128)(2,1)} %constant.4.clone.table_ref.refs_3_) | copy-start | bytes 3145732
  5.3 11.8 %copy-start.8 = (f32[1,1,8]{2,1,0:T(1,128)S(1)}, f32[1,1,8]{2,1,0:T(1,128)}, u32[]{:S(2)}) copy-start(f32[1,1,8]{2,1,0:T(1,128)} %param.17) | copy-start | bytes 100
  5.3 11.8 %copy-start.9 = (f32[1,1,2]{2,1,0:T(1,128)S(1)}, f32[1,1,2]{2,1,0:T(1,128)}, u32[]{:S(2)}) copy-start(f32[1,1,2]{2,1,0:T(1,128)} %param.14) | copy-start | bytes 28
  5.3 12.4 %copy-start.7 = (s32[1,2]{1,0:T(1,128)S(1)}, s32[1,2]{1,0:T(1,128)}, u32[]{:S(2)}) copy-start(s32[1,2]{1,0:T(1,128)} %param.12) | copy-start | bytes 28
  5.3 12.4 %copy-start.10 = (s32[2]{0:T(128)S(1)}, s32[2]{0:T(128)}, u32[]{:S(2)}) copy-start(s32[2]{0:T(128)} %surface_freq_ref.1) | copy-start | bytes 28
  5.3 28.5 %all-to-all-start = ((f32[32,16,256]{2,1,0:T(8,128)}), f32[32,16,256]{2,1,0:T(8,128)S(1)}, u32[]{:S(2)}, u32[]{:S(2)}) async-start(f32[32,16,256]{2,1,0:T(8,128)} %bitcast.2), calls=%async_computation | async-start | bytes 1048576 | tf_op jit(solution)/shard_map/all_to_all | solution.py:424
  17.0 16.8 %copy-start.2 = (bf16[256,1024]{1,0:T(8,128)(2,1)S(1)}, bf16[256,1024]{1,0:T(8,128)(2,1)}, u32[]{:S(2)}) copy-start(bf16[256,1024]{1,0:T(8,128)(2,1)} %constant.5.clone.refs_4_.flip_ref) | copy-start | bytes 1572868
  35.9 18.0 %all-to-all-start.1 = ((f32[8,64,256]{2,1,0:T(8,128)}), f32[8,64,256]{2,1,0:T(8,128)S(1)}, u32[]{:S(2)}, u32[]{:S(2)}) async-start(f32[8,64,256]{2,1,0:T(8,128)} %bitcast.9), calls=%async_computation.1 | async-start | bytes 1048576 | tf_op jit(solution)/shard_map/all_to_all | solution.py:424
  40.7 13.2 %collective-permute-start = (f32[48,512]{1,0:T(8,128)S(1)}, f32[48,512]{1,0:T(8,128)S(1)}, u32[]{:S(2)}, u32[]{:S(2)}) collective-permute-start(f32[48,512]{1,0:T(8,128)S(1)} %get-tuple-element.25.params_ref), channel_id=1, source_target_pairs={{0,224},{32,0},{64,32},{96,64},{128,96},{160,128},{192,160},{224,1... | collective-permute-start | bytes 294920 | tf_op jit(solution)/shard_map/ppermute | solution.py:490
  41.2 10.7 %collective-permute-start.1 = (f32[32,512]{1,0:T(8,128)S(1)}, f32[32,512]{1,0:T(8,128)S(1)}, u32[]{:S(2)}, u32[]{:S(2)}) collective-permute-start(f32[32,512]{1,0:T(8,128)S(1)} %get-tuple-element.29.refs_0_), channel_id=1, source_target_pairs={{0,8},{1,9},{2,10},{3,11},{4,12},{5,13},{6,14},{7,15},{8,16},{9,17... | collective-permute-start | bytes 196616 | tf_op jit(solution)/shard_map/ppermute | solution.py:432
  42.5 9.3 %collective-permute-start.2 = (f32[32,512]{1,0:T(8,128)S(1)}, f32[32,512]{1,0:T(8,128)S(1)}, u32[]{:S(2)}, u32[]{:S(2)}) collective-permute-start(f32[32,512]{1,0:T(8,128)S(1)} %get-tuple-element.29.refs_0_), channel_id=1, source_target_pairs={{0,16},{1,17},{2,18},{3,19},{4,20},{5,21},{6,22},{7,23},{8,24},{9,... | collective-permute-start | bytes 196616 | tf_op jit(solution)/shard_map/ppermute | solution.py:432
  45.2 7.9 %collective-permute-start.3 = (f32[32,512]{1,0:T(8,128)S(1)}, f32[32,512]{1,0:T(8,128)S(1)}, u32[]{:S(2)}, u32[]{:S(2)}) collective-permute-start(f32[32,512]{1,0:T(8,128)S(1)} %get-tuple-element.29.refs_0_), channel_id=1, source_target_pairs={{0,24},{1,25},{2,26},{3,27},{4,28},{5,29},{6,30},{7,31},{8,0},{9,1... | collective-permute-start | bytes 196616 | tf_op jit(solution)/shard_map/ppermute | solution.py:432
  55.8 10.6 %all-to-all-start.2 = ((f32[8,64,128]{2,1,0:T(8,128)}), f32[8,64,128]{2,1,0:T(8,128)S(1)}, u32[]{:S(2)}, u32[]{:S(2)}) async-start(f32[8,64,128]{2,1,0:T(8,128)} %bitcast.11), calls=%async_computation.2 | async-start | bytes 524288 | tf_op jit(solution)/shard_map/all_to_all | solution.py:424
  68.4 39.1 %all-to-all-start.3 = ((f32[32,16,256]{2,1,0:T(8,128)}), f32[32,16,256]{2,1,0:T(8,128)S(1)}, u32[]{:S(2)}, u32[]{:S(2)}) async-start(f32[32,16,256]{2,1,0:T(8,128)} %bitcast.13), calls=%async_computation.3 | async-start | bytes 1048576 | tf_op jit(solution)/shard_map/all_to_all | solution.py:424
  75.4 17.7 %collective-permute-start.4 = (f32[2,16,512]{2,1,0:T(8,128)S(1)}, f32[2,16,512]{2,1,0:T(8,128)S(1)}, u32[]{:S(2)}, u32[]{:S(2)}) collective-permute-start(f32[2,16,512]{2,1,0:T(8,128)S(1)} %get-tuple-element.37), channel_id=1, source_target_pairs={{0,8},{1,9},{2,10},{3,11},{4,12},{5,13},{6,14},{7,15},{8,16},{9,17... | collective-permute-start | bytes 196616 | tf_op jit(solution)/shard_map/ppermute | solution.py:432
  77.9 17.7 %collective-permute-start.5 = (f32[2,16,512]{2,1,0:T(8,128)S(1)}, f32[2,16,512]{2,1,0:T(8,128)S(1)}, u32[]{:S(2)}, u32[]{:S(2)}) collective-permute-start(f32[2,16,512]{2,1,0:T(8,128)S(1)} %get-tuple-element.38), channel_id=1, source_target_pairs={{0,16},{1,17},{2,18},{3,19},{4,20},{5,21},{6,22},{7,23},{8,24},{9,... | collective-permute-start | bytes 196616 | tf_op jit(solution)/shard_map/ppermute | solution.py:432
  81.5 14.1 %collective-permute-start.6 = (f32[2,16,512]{2,1,0:T(8,128)S(1)}, f32[2,16,512]{2,1,0:T(8,128)S(1)}, u32[]{:S(2)}, u32[]{:S(2)}) collective-permute-start(f32[2,16,512]{2,1,0:T(8,128)S(1)} %get-tuple-element.39), channel_id=1, source_target_pairs={{0,24},{1,25},{2,26},{3,27},{4,28},{5,29},{6,30},{7,31},{8,0},{9,1... | collective-permute-start | bytes 196616 | tf_op jit(solution)/shard_map/ppermute | solution.py:432
  95.7 6.9 %collective-permute-start.7 = (f32[8,8,512]{2,1,0:T(8,128)S(1)}, f32[8,8,512]{2,1,0:T(8,128)S(1)}, u32[]{:S(2)}, u32[]{:S(2)}) collective-permute-start(f32[8,8,512]{2,1,0:T(8,128)S(1)} %get-tuple-element.41), channel_id=1, source_target_pairs={{0,1},{1,2},{2,3},{3,4},{4,5},{5,6},{6,7},{7,8},{8,9},{9,10},{10,1... | collective-permute-start | bytes 393224 | tf_op jit(solution)/shard_map/ppermute | solution.py:523
  98.1 9.0 %collective-permute-start.8 = (f32[8,8,512]{2,1,0:T(8,128)S(1)}, f32[8,8,512]{2,1,0:T(8,128)S(1)}, u32[]{:S(2)}, u32[]{:S(2)}) collective-permute-start(f32[8,8,512]{2,1,0:T(8,128)S(1)} %get-tuple-element.42), channel_id=1, source_target_pairs={{1,0},{2,1},{3,2},{4,3},{5,4},{6,5},{7,6},{8,7},{9,8},{10,9},{11,1... | collective-permute-start | bytes 393224 | tf_op jit(solution)/shard_map/ppermute | solution.py:524
  108.2 7.6 %collective-permute-start.9 = (f32[8,16,512]{2,1,0:T(8,128)S(1)}, f32[8,16,512]{2,1,0:T(8,128)S(1)}, u32[]{:S(2)}, u32[]{:S(2)}) collective-permute-start(f32[8,16,512]{2,1,0:T(8,128)S(1)} %get-tuple-element.44), channel_id=1, source_target_pairs={{0,32},{1,33},{2,34},{3,35},{4,36},{5,37},{6,38},{7,39},{8,40},{9,... | collective-permute-start | bytes 786440 | tf_op jit(solution)/shard_map/ppermute | solution.py:559
  108.2 9.0 %collective-permute-start.10 = (f32[8,8,512]{2,1,0:T(8,128)S(1)}, f32[8,8,512]{2,1,0:T(8,128)S(1)}, u32[]{:S(2)}, u32[]{:S(2)}) collective-permute-start(f32[8,8,512]{2,1,0:T(8,128)S(1)} %get-tuple-element.45), channel_id=1, source_target_pairs={{0,33},{1,34},{2,35},{3,36},{4,37},{5,38},{6,39},{7,40},{8,41},{9,... | collective-permute-start | bytes 393224 | tf_op jit(solution)/shard_map/ppermute | solution.py:557
  112.0 10.9 %collective-permute-start.11 = (f32[8,8,512]{2,1,0:T(8,128)S(1)}, f32[8,8,512]{2,1,0:T(8,128)S(1)}, u32[]{:S(2)}, u32[]{:S(2)}) collective-permute-start(f32[8,8,512]{2,1,0:T(8,128)S(1)} %get-tuple-element.46), channel_id=1, source_target_pairs={{1,32},{2,33},{3,34},{4,35},{5,36},{6,37},{7,38},{8,39},{9,40},{10... | collective-permute-start | bytes 393224 | tf_op jit(solution)/shard_map/ppermute | solution.py:558

commit v2 on v1

--- a/solution.py
+++ b/solution.py
@@ -244,7 +244,7 @@
 
 def columns_kernel(*refs, rows, tick):
     in_ref, even_ref, odd_ref, table_ref, flip_ref = refs[:5]
-    out_ref = refs[-1]
+    out_ref = refs[5] if tick == 0 else refs[6]
     table, flipped = Table(table_ref), Table(table_ref, flip_ref)
     length = in_ref.shape[0]
     members = length // rows // GROUPS
@@ -254,10 +254,11 @@
     turn = jnp.where(low, 1.0, -1.0)
     if tick == 0:
         value = in_ref[:, 0:LANES]
+        refs[6][...] = in_ref[:, LANES:]
     else:
         value = jnp.concatenate([in_ref[pl.ds(at * rows, rows), :] for at in order], axis=0)
         at_end = lax.axis_index("depth") == lax.axis_size("depth") - 1
-        value = jnp.where(at_end, refs[5][:, LANES:], value)
+        value = jnp.where(at_end, refs[5][...], value)
     cos_part, sin_part = analysed_left(flipped, value)
     spectrum = cos_part + turn * pltpu.roll(sin_part, CHUNK, 1)
     swapped = pltpu.roll(spectrum, CHUNK, 1)
@@ -387,6 +388,10 @@
     image_body(field_ref, above_ref, below_ref, base_ref, out_ref, padded_ref, rows)
 
 
+def store_kernel(in_ref, out_ref):
+    out_ref[...] = in_ref[...]
+
+
 VMEM = pl.BlockSpec(memory_space=pltpu.VMEM)
 SMEM = pl.BlockSpec(memory_space=pltpu.SMEM)
 
@@ -449,7 +454,7 @@
         return call(
             columns_kernel,
             [VMEM] * (5 + len(more)),
-            [(length, 2 * LANES)],
+            [(length, 2 * LANES)] + [(length, LANES)] * (1 - tick),
             (value, *pair, *tables_x, *more),
             1 << 29,
             rows=rows,
@@ -485,10 +490,10 @@
     entered = exchanged(spectra)
     packed = across([packed] * GROUPS)
     pair = factors(params, 0)
-    shifted = columns(entered, pair, 0)
+    shifted, later = columns(entered, pair, 0)
     returned = exchanged(shifted, groups)
-    passed = lax.ppermute(params, "depth", [(s, (s - 1) % sections) for s in range(sections)])
-    returned, passed = lax.optimization_barrier((returned, passed))
+    upward = [(s, (s - 1) % sections) for s in range(sections)]
+    passed = lax.ppermute(params, "depth", upward)
     weight, lenses = call(
         gather_kernel,
         [SMEM] + [VMEM] * GROUPS,
@@ -497,6 +502,7 @@
         1 << 25,
         rows=rows,
     )
+    next_pair = factors(passed, 1)
     spectra, *pieces = call(
         turn_kernel,
         [VMEM] * 5,
@@ -525,10 +531,8 @@
     image = call(
         image_first, [VMEM] * 3, [image_shape], (parts, above, below), 1 << 26, padded, rows=rows
     )
-    pair = factors(passed, 1)
-    shifted = columns(spectra, pair, 1, entered)
+    shifted = columns(spectra, next_pair, 1, later)
     returned = exchanged(shifted)
-    returned, image = lax.optimization_barrier((returned, image))
     lenses = call(
         lens_kernel,
         [SMEM, SMEM, VMEM],
@@ -566,7 +570,8 @@
         padded,
         rows=rows,
     )
-    return (parts.reshape(fields.shape), image[None, None])
+    stored = call(store_kernel, [VMEM], [parts_shape], (parts,), 1 << 20)
+    return (stored.reshape(fields.shape), image[None, None])
 
 
 def solution(mesh):
@@ -582,4 +587,5 @@
     )
     out_specs = (P("depth", None, None, None, "lat", None), P("depth", None, None, "lat", None))
 
+
     return jax.shard_map(shards, mesh=mesh, in_specs=in_specs, out_specs=out_specs, check_vma=False)

time: 126 us -> 131 us (1.040)
  waiting for transfers between devices: 47.2 us -> 56.6 us
  starting transfers between devices: 58.7 us -> 53.5 us
    all_to_all x4, waiting for transfers between devices: 18.5 us -> 33.6 us  [exchanged(): lax.all_to_all(value, 'lat', split_axis=0, concat_axis=0, tiled=True, axi...]
    ppermute x6, starting transfers between devices: 15.4 us -> 10.7 us  [across(): moved.append(lax.ppermute(pieces[shift], 'lat', pairs))]
    ppermute x1, waiting for transfers between devices: 4.56 us -> 0.01 us  [shards(): below = lax.ppermute(head, 'lat', along(-1))]
    ppermute x6, waiting for transfers between devices: 16.7 us -> 14.1 us  [across(): moved.append(lax.ppermute(pieces[shift], 'lat', pairs))]
    ppermute x1, waiting for transfers between devices: 0.01 us -> 2.21 us  [shards(): passed = lax.ppermute(params, 'depth', upward)]
    pallas_call x13 -> x14, Pallas kernels: 14.2 us -> 15 us  [call(): pl.pallas_call(functools.partial(kernel, **params), in_specs=in_specs, ou...]
    unnamed x23 -> x22, local copies, waits for them, and re-layouts: 3.86 us -> 3.15 us
where the time goes in v2:
time: 131 us; the launch traced here: 129 us
  waiting for transfers between devices  56.6 us (43%)
  starting transfers between devices  53.5 us (41%)
  Pallas kernels  15 us (11%)
  local copies, waits for them, and re-layouts  3.15 us (2%)
    all_to_all x4, waiting for transfers between devices, exchanged(): lax.all_to_all(value, 'lat', split_axis=0, concat_axis=0, tiled=True, axi...  33.6 us
    all_to_all x4, starting transfers between devices, exchanged(): lax.all_to_all(value, 'lat', split_axis=0, concat_axis=0, tiled=True, axi...  30.2 us
    pallas_call x14, Pallas kernels, call(): pl.pallas_call(functools.partial(kernel, **params), in_specs=in_specs, ou...  15 us
    ppermute x6, waiting for transfers between devices, across(): moved.append(lax.ppermute(pieces[shift], 'lat', pairs))  14.1 us
    ppermute x6, starting transfers between devices, across(): moved.append(lax.ppermute(pieces[shift], 'lat', pairs))  10.7 us
    ppermute x1, waiting for transfers between devices, shards(): below = lax.ppermute(head, ('depth', 'lat'), diagonal(-1))  6.14 us
    ppermute x1, starting transfers between devices, shards(): below = lax.ppermute(head, 'lat', along(-1))  3.92 us
    ppermute x1, starting transfers between devices, shards(): above = lax.ppermute(tail, ('depth', 'lat'), diagonal(1))  3.47 us
  transfers between devices with their start and end apart: 16, of which 10 were waited for; matrix products, arithmetic and copies ran while one was open for 0% of the time, Pallas kernels for 4%

profile of v2, /device:TPU:6, one launch (start us, length us, event | category | flops | bytes accessed | tf_op | source)
XLA Modules:
  0.0 129.0 jit_solution(6038530459828440782)
XLA Ops:
  0.6 0.0 copy-start
  0.6 1.2 copy-done
  1.9 0.9 copy-done.3
  2.8 0.9 copy-done.4
  3.8 1.5 %shard_map.113 = f32[512,256]{1,0:T(8,128)} custom-call(f32[128,512]{1,0:T(8,128)S(1)} %bitcast.21, f32[128,512]{1,0:T(8,128)S(1)} %bitcast.22, bf16[256,2048]{1,0:T(8,128)(2,1)S(1)} %copy-done), custom_call_target="tpu_custom_call" | custom-call | flops 268435456 | bytes 1048576 | tf_op jit(solution)/shard_map/pallas_call | solution.py:402
  5.3 0.0 copy-start.10
  5.3 11.7 %all-to-all-start = ((f32[32,16,256]{2,1,0:T(8,128)}), f32[32,16,256]{2,1,0:T(8,128)S(1)}, u32[]{:S(2)}, u32[]{:S(2)}) async-start(f32[32,16,256]{2,1,0:T(8,128)} %bitcast.2), calls=%async_computation | async-start | bytes 1048576 | tf_op jit(solution)/shard_map/all_to_all | solution.py:429
  17.0 0.0 copy-start.2
  17.1 0.6 shard_map.114
  17.7 1.2 shard_map.115
  18.9 14.9 %all-to-all-done = f32[32,16,256]{2,1,0:T(8,128)S(1)} async-done(((f32[32,16,256]{2,1,0:T(8,128)}), f32[32,16,256]{2,1,0:T(8,128)S(1)}, u32[]{:S(2)}, u32[]{:S(2)}) %all-to-all-start) | async-done | bytes 524320 | tf_op jit(solution)/shard_map/all_to_all | solution.py:429
  33.8 2.0 %shard_map.116 = (f32[512,256]{1,0:T(8,128)}, f32[512,128]{1,0:T(8,128)S(1)}) custom-call(f32[512,256]{1,0:T(8,128)S(1)} %bitcast.18, f32[512,128]{1,0:T(8,128)S(1)} %get-tuple-element.24.refs_1_, f32[512,128]{1,0:T(8,128)S(1)} %get-tuple-element.25.refs_2_, bf16[256,2048]{1,0:T(8,128)(2,1)S(1)} %copy-done.1, bf16[256,1024]{1,0:T(8,128)(2,1)S(1)} %copy-done.2), custom_call_target="tpu_custom_call" | custom-call | flops 536870912 | bytes 1048576 | tf_op jit(solution)/shard_map/pallas_call | solution.py:402
  35.9 4.8 %all-to-all-start.1 = ((f32[8,64,256]{2,1,0:T(8,128)}), f32[8,64,256]{2,1,0:T(8,128)S(1)}, u32[]{:S(2)}, u32[]{:S(2)}) async-start(f32[8,64,256]{2,1,0:T(8,128)} %bitcast.9), calls=%async_computation.1 | async-start | bytes 1048576 | tf_op jit(solution)/shard_map/all_to_all | solution.py:429
  40.7 1.5 %collective-permute-start = (f32[32,512]{1,0:T(8,128)S(1)}, f32[32,512]{1,0:T(8,128)S(1)}, u32[]{:S(2)}, u32[]{:S(2)}) collective-permute-start(f32[32,512]{1,0:T(8,128)S(1)} %get-tuple-element.27.refs_0_), channel_id=1, source_target_pairs={{0,8},{1,9},{2,10},{3,11},{4,12},{5,13},{6,14},{7,15},{8,16},{9,17... | collective-permute-start | bytes 196616 | tf_op jit(solution)/shard_map/ppermute | solution.py:437
  42.2 2.0 %collective-permute-start.1 = (f32[32,512]{1,0:T(8,128)S(1)}, f32[32,512]{1,0:T(8,128)S(1)}, u32[]{:S(2)}, u32[]{:S(2)}) collective-permute-start(f32[32,512]{1,0:T(8,128)S(1)} %get-tuple-element.27.refs_0_), channel_id=1, source_target_pairs={{0,16},{1,17},{2,18},{3,19},{4,20},{5,21},{6,22},{7,23},{8,24},{9,... | collective-permute-start | bytes 196616 | tf_op jit(solution)/shard_map/ppermute | solution.py:437
  44.2 2.3 %collective-permute-start.2 = (f32[32,512]{1,0:T(8,128)S(1)}, f32[32,512]{1,0:T(8,128)S(1)}, u32[]{:S(2)}, u32[]{:S(2)}) collective-permute-start(f32[32,512]{1,0:T(8,128)S(1)} %get-tuple-element.27.refs_0_), channel_id=1, source_target_pairs={{0,24},{1,25},{2,26},{3,27},{4,28},{5,29},{6,30},{7,31},{8,0},{9,1... | collective-permute-start | bytes 196616 | tf_op jit(solution)/shard_map/ppermute | solution.py:437
  46.5 5.3 %collective-permute-done.refs_1_ = f32[32,512]{1,0:T(8,128)S(1)} collective-permute-done((f32[32,512]{1,0:T(8,128)S(1)}, f32[32,512]{1,0:T(8,128)S(1)}, u32[]{:S(2)}, u32[]{:S(2)}) %collective-permute-start) | collective-permute-done | bytes 65568 | tf_op jit(solution)/shard_map/ppermute | solution.py:437
  51.9 0.0 collective-permute-done.1.refs_2_
  51.9 0.0 collective-permute-done.2.refs_3_
  51.9 0.8 shard_map.117
  52.6 0.0 all-to-all-done.1
  52.7 1.9 %shard_map.118 = (f32[512,128]{1,0:T(8,128)}, f32[2,16,512]{2,1,0:T(8,128)S(1)}, f32[2,16,512]{2,1,0:T(8,128)S(1)}, f32[2,16,512]{2,1,0:T(8,128)S(1)}, f32[2,16,512]{2,1,0:T(8,128)S(1)}) custom-call(f32[512,256]{1,0:T(8,128)S(1)} %bitcast.17, f32[64,512]{1,0:T(8,128)S(1)} %get-tuple-element.28.weight_ref, f32[2,64,512]{2,1,0:T(8,128)S(1)} %get-tuple-element.29.lens_ref, ...), custom_call_target="tpu_custom_call" | custom-call | flops 536870912 | bytes 1048576 | tf_op jit(solution)/shard_map/pallas_call | solution.py:402
  54.5 5.8 %all-to-all-start.2 = ((f32[8,64,128]{2,1,0:T(8,128)}), f32[8,64,128]{2,1,0:T(8,128)S(1)}, u32[]{:S(2)}, u32[]{:S(2)}) async-start(f32[8,64,128]{2,1,0:T(8,128)} %bitcast.11), calls=%async_computation.2 | async-start | bytes 524288 | tf_op jit(solution)/shard_map/all_to_all | solution.py:429
  60.3 0.0 collective-permute-start.3
  60.3 2.2 %collective-permute-done.3.params_ref.passed_ref = f32[48,512]{1,0:T(8,128)S(1)} collective-permute-done((f32[48,512]{1,0:T(8,128)S(1)}, f32[48,512]{1,0:T(8,128)S(1)}, u32[]{:S(2)}, u32[]{:S(2)}) %collective-permute-start.3) | collective-permute-done | bytes 98336 | tf_op jit(solution)/shard_map/ppermute | solution.py:496
  62.5 1.2 shard_map.119
  63.7 1.4 %all-to-all-done.2 = f32[8,64,128]{2,1,0:T(8,128)S(1)} async-done(((f32[8,64,128]{2,1,0:T(8,128)}), f32[8,64,128]{2,1,0:T(8,128)S(1)}, u32[]{:S(2)}, u32[]{:S(2)}) %all-to-all-start.2) | async-done | bytes 262176 | tf_op jit(solution)/shard_map/all_to_all | solution.py:429
  65.1 2.0 %shard_map.120 = f32[512,256]{1,0:T(8,128)} custom-call(f32[512,128]{1,0:T(8,128)S(1)} %bitcast.20, f32[512,128]{1,0:T(8,128)S(1)} %get-tuple-element.31.refs_1_, f32[512,128]{1,0:T(8,128)S(1)} %get-tuple-element.32.refs_2_, bf16[256,2048]{1,0:T(8,128)(2,1)S(1)} %copy-done.1, bf16[256,1024]{1,0:T(8,128)(2,1)S(1)} %copy-done.2, ...), custom_call_target="tpu_custom_call" | custom-call | flops 536870912 | bytes 1048576 | tf_op jit(solution)/shard_map/pallas_call | solution.py:402
  67.1 7.9 %all-to-all-start.3 = ((f32[32,16,256]{2,1,0:T(8,128)}), f32[32,16,256]{2,1,0:T(8,128)S(1)}, u32[]{:S(2)}, u32[]{:S(2)}) async-start(f32[32,16,256]{2,1,0:T(8,128)} %bitcast.13), calls=%async_computation.3 | async-start | bytes 1048576 | tf_op jit(solution)/shard_map/all_to_all | solution.py:429
  75.1 0.7 shard_map.121.lens_ref
  75.8 17.2 %all-to-all-done.3 = f32[32,16,256]{2,1,0:T(8,128)S(1)} async-done(((f32[32,16,256]{2,1,0:T(8,128)}), f32[32,16,256]{2,1,0:T(8,128)S(1)}, u32[]{:S(2)}, u32[]{:S(2)}) %all-to-all-start.3) | async-done | bytes 524320 | tf_op jit(solution)/shard_map/all_to_all | solution.py:429
  93.0 0.7 shard_map.122
  93.7 0.0 collective-permute-start.4
  93.7 0.8 collective-permute-start.7
  94.5 2.2 %collective-permute-start.8 = (f32[2,16,512]{2,1,0:T(8,128)S(1)}, f32[2,16,512]{2,1,0:T(8,128)S(1)}, u32[]{:S(2)}, u32[]{:S(2)}) collective-permute-start(f32[2,16,512]{2,1,0:T(8,128)S(1)} %get-tuple-element.39), channel_id=1, source_target_pairs={{0,16},{1,17},{2,18},{3,19},{4,20},{5,21},{6,22},{7,23},{8,24},{9,... | collective-permute-start | bytes 196616 | tf_op jit(solution)/shard_map/ppermute | solution.py:437
  96.7 1.9 %collective-permute-start.9 = (f32[2,16,512]{2,1,0:T(8,128)S(1)}, f32[2,16,512]{2,1,0:T(8,128)S(1)}, u32[]{:S(2)}, u32[]{:S(2)}) collective-permute-start(f32[2,16,512]{2,1,0:T(8,128)S(1)} %get-tuple-element.40), channel_id=1, source_target_pairs={{0,24},{1,25},{2,26},{3,27},{4,28},{5,29},{6,30},{7,31},{8,0},{9,1... | collective-permute-start | bytes 196616 | tf_op jit(solution)/shard_map/ppermute | solution.py:437
  98.6 1.7 %collective-permute-done.7.refs_1_ = f32[2,16,512]{2,1,0:T(8,128)S(1)} collective-permute-done((f32[2,16,512]{2,1,0:T(8,128)S(1)}, f32[2,16,512]{2,1,0:T(8,128)S(1)}, u32[]{:S(2)}, u32[]{:S(2)}) %collective-permute-start.7) | collective-permute-done | bytes 65568 | tf_op jit(solution)/shard_map/ppermute | solution.py:437
  100.3 3.2 %collective-permute-done.8.refs_2_ = f32[2,16,512]{2,1,0:T(8,128)S(1)} collective-permute-done((f32[2,16,512]{2,1,0:T(8,128)S(1)}, f32[2,16,512]{2,1,0:T(8,128)S(1)}, u32[]{:S(2)}, u32[]{:S(2)}) %collective-permute-start.8) | collective-permute-done | bytes 65568 | tf_op jit(solution)/shard_map/ppermute | solution.py:437
  103.5 3.8 %collective-permute-done.9.refs_3_ = f32[2,16,512]{2,1,0:T(8,128)S(1)} collective-permute-done((f32[2,16,512]{2,1,0:T(8,128)S(1)}, f32[2,16,512]{2,1,0:T(8,128)S(1)}, u32[]{:S(2)}, u32[]{:S(2)}) %collective-permute-start.9) | collective-permute-done | bytes 65568 | tf_op jit(solution)/shard_map/ppermute | solution.py:437
  107.4 1.9 %collective-permute-start.10 = (f32[8,8,512]{2,1,0:T(8,128)S(1)}, f32[8,8,512]{2,1,0:T(8,128)S(1)}, u32[]{:S(2)}, u32[]{:S(2)}) collective-permute-start(f32[8,8,512]{2,1,0:T(8,128)S(1)} %get-tuple-element.42), channel_id=1, source_target_pairs={{0,1},{1,2},{2,3},{3,4},{4,5},{5,6},{6,7},{7,8},{8,9},{9,10},{10,1... | collective-permute-start | bytes 393224 | tf_op jit(solution)/shard_map/ppermute | solution.py:529
  109.3 3.9 %collective-permute-start.11 = (f32[8,8,512]{2,1,0:T(8,128)S(1)}, f32[8,8,512]{2,1,0:T(8,128)S(1)}, u32[]{:S(2)}, u32[]{:S(2)}) collective-permute-start(f32[8,8,512]{2,1,0:T(8,128)S(1)} %get-tuple-element.43), channel_id=1, source_target_pairs={{1,0},{2,1},{3,2},{4,3},{5,4},{6,5},{7,6},{8,7},{9,8},{10,9},{11,1... | collective-permute-start | bytes 393224 | tf_op jit(solution)/shard_map/ppermute | solution.py:530
  113.2 3.5 %collective-permute-start.5 = (f32[8,8,512]{2,1,0:T(8,128)S(1)}, f32[8,8,512]{2,1,0:T(8,128)S(1)}, u32[]{:S(2)}, u32[]{:S(2)}) collective-permute-start(f32[8,8,512]{2,1,0:T(8,128)S(1)} %get-tuple-element.35), channel_id=1, source_target_pairs={{0,33},{1,34},{2,35},{3,36},{4,37},{5,38},{6,39},{7,40},{8,41},{9,... | collective-permute-start | bytes 393224 | tf_op jit(solution)/shard_map/ppermute | solution.py:561
  116.7 3.2 %collective-permute-start.6 = (f32[8,8,512]{2,1,0:T(8,128)S(1)}, f32[8,8,512]{2,1,0:T(8,128)S(1)}, u32[]{:S(2)}, u32[]{:S(2)}) collective-permute-start(f32[8,8,512]{2,1,0:T(8,128)S(1)} %get-tuple-element.36), channel_id=1, source_target_pairs={{1,32},{2,33},{3,34},{4,35},{5,36},{6,37},{7,38},{8,39},{9,40},{10... | collective-permute-start | bytes 393224 | tf_op jit(solution)/shard_map/ppermute | solution.py:562
  119.9 0.4 shard_map.125.base_ref
  120.3 0.7 shard_map.123
  121.0 0.6 collective-permute-done.5.above_ref
  121.6 6.1 %collective-permute-done.6.below_ref = f32[8,8,512]{2,1,0:T(8,128)S(1)} collective-permute-done((f32[8,8,512]{2,1,0:T(8,128)S(1)}, f32[8,8,512]{2,1,0:T(8,128)S(1)}, u32[]{:S(2)}, u32[]{:S(2)}) %collective-permute-start.6) | collective-permute-done | bytes 131104 | tf_op jit(solution)/shard_map/ppermute | solution.py:562
  127.8 1.3 shard_map.126
  (20 shorter events, 0.1 us)
Async XLA Ops:
  0.6 1.2 copy-start
  1.9 0.9 copy-start.3
  2.8 0.9 copy-start.4
  3.8 13.3 %copy-start.5 = (s32[1,1,16,512]{3,2,1,0:T(8,128)S(1)}, s32[1,1,16,512]{3,2,1,0:T(8,128)}, u32[]{:S(2)}) copy-start(s32[1,1,16,512]{3,2,1,0:T(8,128)} %param.16) | copy-start | bytes 98308
  3.8 13.3 %copy-start.6 = (f32[1,1,16,512]{3,2,1,0:T(8,128)S(1)}, f32[1,1,16,512]{3,2,1,0:T(8,128)}, u32[]{:S(2)}) copy-start(f32[1,1,16,512]{3,2,1,0:T(8,128)} %param.15) | copy-start | bytes 98308
  5.3 28.6 %copy-start.1 = (bf16[256,2048]{1,0:T(8,128)(2,1)S(1)}, bf16[256,2048]{1,0:T(8,128)(2,1)}, u32[]{:S(2)}) copy-start(bf16[256,2048]{1,0:T(8,128)(2,1)} %constant.4.clone.table_ref.refs_3_) | copy-start | bytes 3145732
  5.3 11.8 %copy-start.8 = (f32[1,1,8]{2,1,0:T(1,128)S(1)}, f32[1,1,8]{2,1,0:T(1,128)}, u32[]{:S(2)}) copy-start(f32[1,1,8]{2,1,0:T(1,128)} %param.17) | copy-start | bytes 100
  5.3 11.8 %copy-start.9 = (f32[1,1,2]{2,1,0:T(1,128)S(1)}, f32[1,1,2]{2,1,0:T(1,128)}, u32[]{:S(2)}) copy-start(f32[1,1,2]{2,1,0:T(1,128)} %param.14) | copy-start | bytes 28
  5.3 12.4 %copy-start.7 = (s32[1,2]{1,0:T(1,128)S(1)}, s32[1,2]{1,0:T(1,128)}, u32[]{:S(2)}) copy-start(s32[1,2]{1,0:T(1,128)} %param.12) | copy-start | bytes 28
  5.3 12.4 %copy-start.10 = (s32[2]{0:T(128)S(1)}, s32[2]{0:T(128)}, u32[]{:S(2)}) copy-start(s32[2]{0:T(128)} %surface_freq_ref.1) | copy-start | bytes 28
  5.3 28.5 %all-to-all-start = ((f32[32,16,256]{2,1,0:T(8,128)}), f32[32,16,256]{2,1,0:T(8,128)S(1)}, u32[]{:S(2)}, u32[]{:S(2)}) async-start(f32[32,16,256]{2,1,0:T(8,128)} %bitcast.2), calls=%async_computation | async-start | bytes 1048576 | tf_op jit(solution)/shard_map/all_to_all | solution.py:429
  17.0 16.8 %copy-start.2 = (bf16[256,1024]{1,0:T(8,128)(2,1)S(1)}, bf16[256,1024]{1,0:T(8,128)(2,1)}, u32[]{:S(2)}) copy-start(bf16[256,1024]{1,0:T(8,128)(2,1)} %constant.5.clone.refs_4_.flip_ref) | copy-start | bytes 1572868
  35.9 16.8 %all-to-all-start.1 = ((f32[8,64,256]{2,1,0:T(8,128)}), f32[8,64,256]{2,1,0:T(8,128)S(1)}, u32[]{:S(2)}, u32[]{:S(2)}) async-start(f32[8,64,256]{2,1,0:T(8,128)} %bitcast.9), calls=%async_computation.1 | async-start | bytes 1048576 | tf_op jit(solution)/shard_map/all_to_all | solution.py:429
  40.7 11.1 %collective-permute-start = (f32[32,512]{1,0:T(8,128)S(1)}, f32[32,512]{1,0:T(8,128)S(1)}, u32[]{:S(2)}, u32[]{:S(2)}) collective-permute-start(f32[32,512]{1,0:T(8,128)S(1)} %get-tuple-element.27.refs_0_), channel_id=1, source_target_pairs={{0,8},{1,9},{2,10},{3,11},{4,12},{5,13},{6,14},{7,15},{8,16},{9,17... | collective-permute-start | bytes 196616 | tf_op jit(solution)/shard_map/ppermute | solution.py:437
  42.2 9.7 %collective-permute-start.1 = (f32[32,512]{1,0:T(8,128)S(1)}, f32[32,512]{1,0:T(8,128)S(1)}, u32[]{:S(2)}, u32[]{:S(2)}) collective-permute-start(f32[32,512]{1,0:T(8,128)S(1)} %get-tuple-element.27.refs_0_), channel_id=1, source_target_pairs={{0,16},{1,17},{2,18},{3,19},{4,20},{5,21},{6,22},{7,23},{8,24},{9,... | collective-permute-start | bytes 196616 | tf_op jit(solution)/shard_map/ppermute | solution.py:437
  44.2 7.7 %collective-permute-start.2 = (f32[32,512]{1,0:T(8,128)S(1)}, f32[32,512]{1,0:T(8,128)S(1)}, u32[]{:S(2)}, u32[]{:S(2)}) collective-permute-start(f32[32,512]{1,0:T(8,128)S(1)} %get-tuple-element.27.refs_0_), channel_id=1, source_target_pairs={{0,24},{1,25},{2,26},{3,27},{4,28},{5,29},{6,30},{7,31},{8,0},{9,1... | collective-permute-start | bytes 196616 | tf_op jit(solution)/shard_map/ppermute | solution.py:437
  54.5 10.6 %all-to-all-start.2 = ((f32[8,64,128]{2,1,0:T(8,128)}), f32[8,64,128]{2,1,0:T(8,128)S(1)}, u32[]{:S(2)}, u32[]{:S(2)}) async-start(f32[8,64,128]{2,1,0:T(8,128)} %bitcast.11), calls=%async_computation.2 | async-start | bytes 524288 | tf_op jit(solution)/shard_map/all_to_all | solution.py:429
  60.3 2.2 %collective-permute-start.3 = (f32[48,512]{1,0:T(8,128)S(1)}, f32[48,512]{1,0:T(8,128)S(1)}, u32[]{:S(2)}, u32[]{:S(2)}) collective-permute-start(f32[48,512]{1,0:T(8,128)S(1)} %get-tuple-element.23.params_ref), channel_id=1, source_target_pairs={{0,224},{32,0},{64,32},{96,64},{128,96},{160,128},{192,160},{224,1... | collective-permute-start | bytes 294920 | tf_op jit(solution)/shard_map/ppermute | solution.py:496
  67.1 25.9 %all-to-all-start.3 = ((f32[32,16,256]{2,1,0:T(8,128)}), f32[32,16,256]{2,1,0:T(8,128)S(1)}, u32[]{:S(2)}, u32[]{:S(2)}) async-start(f32[32,16,256]{2,1,0:T(8,128)} %bitcast.13), calls=%async_computation.3 | async-start | bytes 1048576 | tf_op jit(solution)/shard_map/all_to_all | solution.py:429
  93.7 26.6 %collective-permute-start.4 = (f32[8,16,512]{2,1,0:T(8,128)S(1)}, f32[8,16,512]{2,1,0:T(8,128)S(1)}, u32[]{:S(2)}, u32[]{:S(2)}) collective-permute-start(f32[8,16,512]{2,1,0:T(8,128)S(1)} %get-tuple-element.34), channel_id=1, source_target_pairs={{0,32},{1,33},{2,34},{3,35},{4,36},{5,37},{6,38},{7,39},{8,40},{9,... | collective-permute-start | bytes 786440 | tf_op jit(solution)/shard_map/ppermute | solution.py:563
  93.7 6.6 %collective-permute-start.7 = (f32[2,16,512]{2,1,0:T(8,128)S(1)}, f32[2,16,512]{2,1,0:T(8,128)S(1)}, u32[]{:S(2)}, u32[]{:S(2)}) collective-permute-start(f32[2,16,512]{2,1,0:T(8,128)S(1)} %get-tuple-element.38), channel_id=1, source_target_pairs={{0,8},{1,9},{2,10},{3,11},{4,12},{5,13},{6,14},{7,15},{8,16},{9,17... | collective-permute-start | bytes 196616 | tf_op jit(solution)/shard_map/ppermute | solution.py:437
  94.5 9.0 %collective-permute-start.8 = (f32[2,16,512]{2,1,0:T(8,128)S(1)}, f32[2,16,512]{2,1,0:T(8,128)S(1)}, u32[]{:S(2)}, u32[]{:S(2)}) collective-permute-start(f32[2,16,512]{2,1,0:T(8,128)S(1)} %get-tuple-element.39), channel_id=1, source_target_pairs={{0,16},{1,17},{2,18},{3,19},{4,20},{5,21},{6,22},{7,23},{8,24},{9,... | collective-permute-start | bytes 196616 | tf_op jit(solution)/shard_map/ppermute | solution.py:437
  96.7 10.6 %collective-permute-start.9 = (f32[2,16,512]{2,1,0:T(8,128)S(1)}, f32[2,16,512]{2,1,0:T(8,128)S(1)}, u32[]{:S(2)}, u32[]{:S(2)}) collective-permute-start(f32[2,16,512]{2,1,0:T(8,128)S(1)} %get-tuple-element.40), channel_id=1, source_target_pairs={{0,24},{1,25},{2,26},{3,27},{4,28},{5,29},{6,30},{7,31},{8,0},{9,1... | collective-permute-start | bytes 196616 | tf_op jit(solution)/shard_map/ppermute | solution.py:437
  107.4 12.5 %collective-permute-start.10 = (f32[8,8,512]{2,1,0:T(8,128)S(1)}, f32[8,8,512]{2,1,0:T(8,128)S(1)}, u32[]{:S(2)}, u32[]{:S(2)}) collective-permute-start(f32[8,8,512]{2,1,0:T(8,128)S(1)} %get-tuple-element.42), channel_id=1, source_target_pairs={{0,1},{1,2},{2,3},{3,4},{4,5},{5,6},{6,7},{7,8},{8,9},{9,10},{10,1... | collective-permute-start | bytes 393224 | tf_op jit(solution)/shard_map/ppermute | solution.py:529
  109.3 10.6 %collective-permute-start.11 = (f32[8,8,512]{2,1,0:T(8,128)S(1)}, f32[8,8,512]{2,1,0:T(8,128)S(1)}, u32[]{:S(2)}, u32[]{:S(2)}) collective-permute-start(f32[8,8,512]{2,1,0:T(8,128)S(1)} %get-tuple-element.43), channel_id=1, source_target_pairs={{1,0},{2,1},{3,2},{4,3},{5,4},{6,5},{7,6},{8,7},{9,8},{10,9},{11,1... | collective-permute-start | bytes 393224 | tf_op jit(solution)/shard_map/ppermute | solution.py:530
  113.2 8.4 %collective-permute-start.5 = (f32[8,8,512]{2,1,0:T(8,128)S(1)}, f32[8,8,512]{2,1,0:T(8,128)S(1)}, u32[]{:S(2)}, u32[]{:S(2)}) collective-permute-start(f32[8,8,512]{2,1,0:T(8,128)S(1)} %get-tuple-element.35), channel_id=1, source_target_pairs={{0,33},{1,34},{2,35},{3,36},{4,37},{5,38},{6,39},{7,40},{8,41},{9,... | collective-permute-start | bytes 393224 | tf_op jit(solution)/shard_map/ppermute | solution.py:561
  116.7 11.1 %collective-permute-start.6 = (f32[8,8,512]{2,1,0:T(8,128)S(1)}, f32[8,8,512]{2,1,0:T(8,128)S(1)}, u32[]{:S(2)}, u32[]{:S(2)}) collective-permute-start(f32[8,8,512]{2,1,0:T(8,128)S(1)} %get-tuple-element.36), channel_id=1, source_target_pairs={{1,32},{2,33},{3,34},{4,35},{5,36},{6,37},{7,38},{8,39},{9,40},{10... | collective-permute-start | bytes 393224 | tf_op jit(solution)/shard_map/ppermute | solution.py:562
